TPU v7x, 16 devices: a whole 2x2x2 slice. The times are simulated.
16 devices in a mesh: data: 2 (over z), seq: 8 (over y, x, core).
Axes of the slice: x: 2, y: 2, z: 2, core: 2. Of those that a mesh axis runs over, the one named last changes fastest.
Arguments:
- x_in: bfloat16 [16, 1024, 2048], P(None, ('data', 'seq')), parts along dimension 1
- positions: int32 [1024], P(('data', 'seq')), parts along dimension 0
- w_query: bfloat16 [3, 2048, 32, 64], replicated
- w_key: bfloat16 [3, 2048, 8, 64], replicated
- w_value: bfloat16 [3, 2048, 8, 64], replicated
- w_out: bfloat16 [3, 32, 64, 2048], replicated
- w_up: bfloat16 [3, 2048, 8192], replicated
- w_down: bfloat16 [3, 8192, 2048], replicated
- g_attn: float32 [3, 2048], replicated
- g_mlp: float32 [3, 2048], replicated
Outputs:
- output: bfloat16 [16, 1024, 2048], P(None, ('data', 'seq')), parts along dimension 1
There are 2 independent parts. A program takes and returns all parts, laid end to end along the dimension named above; an argument that names none is the same for every part.
All inputs are finite; a program needn't handle non-finite values.
Results may differ from a plain program's by a relative error of at most 0.0166204.
Values are sent between devices in bfloat16 or wider.
A program may use at most 1.25 GiB of HBM per device.

v0:
```python
import jax
import jax.numpy as jnp
from jax import lax
from jax.sharding import PartitionSpec as P

ROPE_BASE = 10000.0
NORM_EPS = 1e-6


def rms_norm(x_act, gain_vec):
    x_f32 = x_act.astype(jnp.float32)
    mean_sq = jnp.mean(x_f32 * x_f32, axis=-1, keepdims=True)
    return (x_f32 * lax.rsqrt(mean_sq + NORM_EPS) * gain_vec).astype(jnp.bfloat16)


def rope_tables(positions, head_dim):
    inv_freq = ROPE_BASE ** (-jnp.arange(head_dim // 2, dtype=jnp.float32) * (2.0 / head_dim))
    angles = positions.astype(jnp.float32)[..., None] * inv_freq
    return jnp.cos(angles), jnp.sin(angles)


def apply_rope(proj_f32, cos_t, sin_t):
    half_dim = proj_f32.shape[-1] // 2
    x_first = proj_f32[..., :half_dim]
    x_second = proj_f32[..., half_dim:]
    cos_b = cos_t[..., None, :]
    sin_b = sin_t[..., None, :]
    return jnp.concatenate([x_first * cos_b - x_second * sin_b, x_second * cos_b + x_first * sin_b], axis=-1).astype(jnp.bfloat16)


def causal_attention(q_heads, k_heads, v_heads, q_offset, q_block):
    n_batch, q_len, kv_heads, groups, head_dim = q_heads.shape
    key_len = k_heads.shape[1]
    n_blocks = q_len // q_block
    att_scale = head_dim ** -0.5
    key_pos = jnp.arange(key_len)

    def one_block(blk_idx):
        blk_start = blk_idx * q_block
        q_blk = lax.dynamic_slice_in_dim(q_heads, blk_start, q_block, axis=1)
        scores = jnp.einsum("bqkgd,bskd->bkgqs", q_blk, k_heads, preferred_element_type=jnp.float32) * att_scale
        query_pos = q_offset + blk_start + jnp.arange(q_block)
        scores = jnp.where(key_pos[None, :] <= query_pos[:, None], scores, -1e30)
        row_max = jnp.max(scores, axis=-1, keepdims=True)
        exp_f32 = jnp.exp(scores - row_max)
        row_sum = jnp.sum(exp_f32, axis=-1)
        weighted = jnp.einsum("bkgqs,bskd->bqkgd", exp_f32.astype(jnp.bfloat16), v_heads, preferred_element_type=jnp.float32)
        return (weighted / jnp.transpose(row_sum, (0, 3, 1, 2))[..., None]).astype(jnp.bfloat16)

    blocks = lax.map(one_block, jnp.arange(n_blocks))
    return jnp.moveaxis(blocks, 0, 1).reshape(n_batch, q_len, kv_heads * groups, head_dim)


def layer_step(hidden, cos_t, sin_t, w_query, w_key, w_value, w_out, w_up, w_down, gain_attn, gain_mlp):
    normed = rms_norm(hidden, gain_attn)
    q_loc = apply_rope(jnp.einsum("bsd,dhe->bshe", normed, w_query, preferred_element_type=jnp.float32), cos_t, sin_t)
    k_loc = apply_rope(jnp.einsum("bsd,dhe->bshe", normed, w_key, preferred_element_type=jnp.float32), cos_t, sin_t)
    v_loc = jnp.einsum("bsd,dhe->bshe", normed, w_value, preferred_element_type=jnp.float32).astype(jnp.bfloat16)
    q_all = lax.all_to_all(q_loc, "seq", 2, 1, tiled=True)
    k_all = lax.all_to_all(k_loc, "seq", 2, 1, tiled=True)
    v_all = lax.all_to_all(v_loc, "seq", 2, 1, tiled=True)
    n_batch, seq_len, heads_loc, head_dim = q_all.shape
    kv_loc = k_all.shape[2]
    q_grouped = q_all.reshape(n_batch, seq_len, kv_loc, heads_loc // kv_loc, head_dim)
    attn_heads = causal_attention(q_grouped, k_all, v_all, 0, min(256, seq_len))
    attn_loc = lax.all_to_all(attn_heads, "seq", 1, 2, tiled=True)
    resid_h = (hidden.astype(jnp.float32) + jnp.einsum("bshe,hed->bsd", attn_loc, w_out, preferred_element_type=jnp.float32)).astype(jnp.bfloat16)
    normed_mlp = rms_norm(resid_h, gain_mlp)
    gelu_act = jax.nn.gelu(jnp.einsum("bsd,df->bsf", normed_mlp, w_up, preferred_element_type=jnp.float32), approximate=True).astype(jnp.bfloat16)
    layer_out = resid_h.astype(jnp.float32) + jnp.einsum("bsf,fd->bsd", gelu_act, w_down, preferred_element_type=jnp.float32)
    return layer_out.astype(jnp.bfloat16)


def solution(mesh):
    tok_spec = P(None, ("data", "seq"), None)
    in_specs = (tok_spec, P(("data", "seq"))) + (P(),) * 8

    def device_fn(x_loc, pos_loc, w_query, w_key, w_value, w_out, w_up, w_down, g_attn, g_mlp):
        cos_t, sin_t = rope_tables(pos_loc, w_query.shape[-1])
        hidden = x_loc
        for layer_idx in range(w_query.shape[0]):
            hidden = layer_step(hidden, cos_t, sin_t, w_query[layer_idx], w_key[layer_idx], w_value[layer_idx], w_out[layer_idx], w_up[layer_idx], w_down[layer_idx], g_attn[layer_idx], g_mlp[layer_idx])
        return hidden

    return jax.shard_map(device_fn, mesh=mesh, in_specs=in_specs, out_specs=tok_spec, check_vma=False)
```

profile of v0, /device:TPU:0, one launch (start us, length us, event | category | flops | bytes accessed | tf_op | source)
XLA Modules:
  0.0 1470.8 jit_solution(13211302937985277837)
XLA Ops:
  21.8 23.4 %fusion.166 = f32[16,64,32,64]{1,3,2,0:T(8,128)} fusion(bf16[3,2048,32,64]{1,3,2,0:T(8,128)(2,1)} %param.18, bf16[16,64,2048]{2,1,0:T(8,128)(2,1)} %param.16, f32[2048]{0:T(1024)S(1)} %bitcast.599, f32[16,64]{1,0:T(8,128)S(1)} %add_rsqrt_fusion.5), kind=kOutput, calls=%fused_computation.175 | convolution fusion | flops 8598323200 | bytes 20983808 | tf_op jit(solution)/shard_map/bsd,dhe->bshe/dot_general | solution.py:56
  100.7 34.3 %all-to-all-done = bf16[8,2,131072]{2,1,0:T(2,128)(2,1)} async-done(((bf16[8,2,131072]{2,1,0:T(2,128)(2,1)}), bf16[8,2,131072]{2,1,0:T(2,128)(2,1)}, u32[]{:S(2)}, u32[]{:S(2)}) %all-to-all-start) | async-done | bytes 4194336 | tf_op jit(solution)/shard_map/all_to_all | solution.py:59
  145.8 23.6 %copy.60 = bf16[16,8,64,4,64]{2,1,4,3,0:T(8,128)(2,1)} copy(bf16[16,8,64,4,64]{2,4,0,3,1:T(8,128)(2,1)} %bitcast.575) | data formatting | bytes 8388608 | tf_op jit(solution)/shard_map/all_to_all | solution.py:59
  183.9 94.0 %while.33 = (s32[]{:T(128)}, bf16[2,16,256,1,4,64]{2,5,4,1,3,0:T(8,128)(2,1)}, s32[2]{0:T(128)S(1)}, bf16[16,512,1,4,64]{1,4,3,0,2:T(8,128)(2,1)}, bf16[16,512,1...) while((s32[]{:T(128)}, ...), condition=%wide.region_4.5_spmd.clone, body=%wide.region_1.4_spmd.clone.sunk | while | flops 2241954048 | bytes 107809448 | solution.py:50
  307.8 48.4 %all-to-all-done.3 = bf16[8,2,131072]{2,1,0:T(2,128)(2,1)} async-done(((bf16[8,2,131072]{2,1,0:T(2,128)(2,1)}), bf16[8,2,131072]{2,1,0:T(2,128)(2,1)}, u32[]{:S(2)}, u32[]{:S(2)}) %all-to-all-start.3) | async-done | bytes 4194336 | tf_op jit(solution)/shard_map/all_to_all | solution.py:66
  366.5 16.5 %copy.103 = bf16[16,8,64,4,64]{4,2,3,1,0:T(8,128)(2,1)} copy(bf16[16,8,64,4,64]{4,3,0,2,1:T(4,128)(2,1)} %bitcast.576) | data formatting | bytes 8388608 | tf_op jit(solution)/shard_map/all_to_all | solution.py:66
  398.5 47.0 %fusion.205.clone.5 = bf16[16,64,8192]{2,1,0:T(8,128)(2,1)} fusion(bf16[3,2048,8192]{2,1,0:T(8,128)(2,1)} %param.22, bf16[16,64,2048]{2,1,0:T(8,128)(2,1)} %get-tuple-element.260, f32[2048]{0:T(1024)S(1)} %bitcast.601, f32[16,64]{1,0:T(8,128)S(1)} %add_rsqrt_fusion.4), kind=kOutput, calls=%fused_computation.76.clone.clone.clone.clone.clone.clone.2 | convolution fusion | flops 34443624448 | bytes 54538240 | tf_op jit(solution)/shard_map/bsd,df->bsf/dot_general | solution.py:69
  445.6 45.4 %fusion.140 = (f32[16,64]{1,0:T(8,128)S(1)}, bf16[16,64,2048]{2,1,0:T(8,128)(2,1)}) fusion(bf16[3,8192,2048]{2,1,0:T(8,128)(2,1)} %param.23, bf16[16,64,2048]{2,1,0:T(8,128)(2,1)} %get-tuple-element.260, bf16[16,64,8192]{2,1,0:T(8,128)(2,1)} %fusion.205.clone.5), kind=kOutput, calls=%fused_computation.146 | convolution fusion | flops 34372321280 | bytes 58724352 | tf_op jit(solution)/shard_map/bsf,fd->bsd/dot_general | solution.py:70
  501.0 22.8 %fusion.162 = f32[16,64,32,64]{1,3,2,0:T(8,128)} fusion(bf16[3,2048,32,64]{1,3,2,0:T(8,128)(2,1)S(1)} %copy-done.21, bf16[16,64,2048]{2,1,0:T(8,128)(2,1)} %get-tuple-element.262, f32[2048]{0:T(1024)S(1)} %bitcast.595, f32[16,64]{1,0:T(8,128)S(1)} %add_rsqrt_fusion.3), kind=kOutput, calls=%fused_computation.171 | convolution fusion | flops 8598323200 | bytes 20987904 | tf_op jit(solution)/shard_map/bsd,dhe->bshe/dot_general | solution.py:56
  589.7 35.9 %all-to-all-done.4 = bf16[8,2,131072]{2,1,0:T(2,128)(2,1)} async-done(((bf16[8,2,131072]{2,1,0:T(2,128)(2,1)}), bf16[8,2,131072]{2,1,0:T(2,128)(2,1)}, u32[]{:S(2)}, u32[]{:S(2)}) %all-to-all-start.4) | async-done | bytes 4194336 | tf_op jit(solution)/shard_map/all_to_all | solution.py:59
  636.2 23.6 %copy.70 = bf16[16,8,64,4,64]{2,1,4,3,0:T(8,128)(2,1)} copy(bf16[16,8,64,4,64]{2,4,0,3,1:T(8,128)(2,1)} %bitcast.577) | data formatting | bytes 8388608 | tf_op jit(solution)/shard_map/all_to_all | solution.py:59
  674.2 94.1 %while.34 = (s32[]{:T(128)}, bf16[2,16,256,1,4,64]{2,5,4,1,3,0:T(8,128)(2,1)}, s32[2]{0:T(128)S(1)}, bf16[16,512,1,4,64]{1,4,3,0,2:T(8,128)(2,1)}, bf16[16,512,1...) while((s32[]{:T(128)}, ...), condition=%wide.region_10.11_spmd.clone, body=%wide.region_7.10_spmd.clone.sunk | while | flops 2241954048 | bytes 107809448 | solution.py:50
  792.6 53.5 %all_to_all.207 = bf16[8,2,131072]{2,1,0:T(2,128)(2,1)} all-to-all(bf16[8,2,131072]{2,1,0:T(2,128)(2,1)} %reshape.290), channel_id=1, replica_groups=mesh['data'=2,'seq'=8] {'seq'}, dimensions={0} | all-to-all | bytes 8388608 | tf_op jit(solution)/shard_map/all_to_all | solution.py:66
  856.4 16.5 %copy.106 = bf16[16,8,64,4,64]{4,2,3,1,0:T(8,128)(2,1)} copy(bf16[16,8,64,4,64]{4,3,0,2,1:T(4,128)(2,1)} %bitcast.578) | data formatting | bytes 8388608 | tf_op jit(solution)/shard_map/all_to_all | solution.py:66
  888.5 47.0 %fusion.194.clone.5 = bf16[16,64,8192]{2,1,0:T(8,128)(2,1)} fusion(bf16[3,2048,8192]{2,1,0:T(8,128)(2,1)} %param.22, bf16[16,64,2048]{2,1,0:T(8,128)(2,1)} %get-tuple-element.264, f32[2048]{0:T(1024)S(1)} %bitcast.597, f32[16,64]{1,0:T(8,128)S(1)} %add_rsqrt_fusion.2), kind=kOutput, calls=%fused_computation.84.clone.clone.clone.clone.clone.clone.2 | convolution fusion | flops 34443624448 | bytes 54538240 | tf_op jit(solution)/shard_map/bsd,df->bsf/dot_general | solution.py:69
  935.5 45.5 %fusion.148 = (f32[16,64]{1,0:T(8,128)S(1)}, bf16[16,64,2048]{2,1,0:T(8,128)(2,1)}) fusion(bf16[3,8192,2048]{2,1,0:T(8,128)(2,1)} %param.23, bf16[16,64,2048]{2,1,0:T(8,128)(2,1)} %get-tuple-element.264, bf16[16,64,8192]{2,1,0:T(8,128)(2,1)} %fusion.194.clone.5), kind=kOutput, calls=%fused_computation.154 | convolution fusion | flops 34372321280 | bytes 58724352 | tf_op jit(solution)/shard_map/bsf,fd->bsd/dot_general | solution.py:70
  991.1 22.8 %fusion.158 = f32[16,64,32,64]{1,3,2,0:T(8,128)} fusion(bf16[3,2048,32,64]{1,3,2,0:T(8,128)(2,1)S(1)} %copy-done.22, bf16[16,64,2048]{2,1,0:T(8,128)(2,1)} %get-tuple-element.266, f32[2048]{0:T(1024)S(1)} %bitcast.591, f32[16,64]{1,0:T(8,128)S(1)} %add_rsqrt_fusion.1), kind=kOutput, calls=%fused_computation.167 | convolution fusion | flops 8598323200 | bytes 20987904 | tf_op jit(solution)/shard_map/bsd,dhe->bshe/dot_general | solution.py:56
  1079.6 35.9 %all-to-all-done.8 = bf16[8,2,131072]{2,1,0:T(2,128)(2,1)} async-done(((bf16[8,2,131072]{2,1,0:T(2,128)(2,1)}), bf16[8,2,131072]{2,1,0:T(2,128)(2,1)}, u32[]{:S(2)}, u32[]{:S(2)}) %all-to-all-start.8) | async-done | bytes 4194336 | tf_op jit(solution)/shard_map/all_to_all | solution.py:59
  1126.1 23.8 %copy.80 = bf16[16,8,64,4,64]{2,1,4,3,0:T(8,128)(2,1)} copy(bf16[16,8,64,4,64]{2,4,0,3,1:T(8,128)(2,1)} %bitcast.579) | data formatting | bytes 8388608 | tf_op jit(solution)/shard_map/all_to_all | solution.py:59
  1164.4 93.9 %while.35 = (s32[]{:T(128)}, bf16[2,16,256,1,4,64]{2,5,4,1,3,0:T(8,128)(2,1)}, s32[2]{0:T(128)S(1)}, bf16[16,512,1,4,64]{1,4,3,0,2:T(8,128)(2,1)}, bf16[16,512,1...) while((s32[]{:T(128)}, ...), condition=%wide.region_16.17_spmd.clone, body=%wide.region_13.16_spmd.clone.sunk | while | flops 2241954048 | bytes 107809448 | solution.py:50
  1282.5 53.5 %all_to_all.208 = bf16[8,2,131072]{2,1,0:T(2,128)(2,1)} all-to-all(bf16[8,2,131072]{2,1,0:T(2,128)(2,1)} %reshape.298), channel_id=1, replica_groups=mesh['data'=2,'seq'=8] {'seq'}, dimensions={0} | all-to-all | bytes 8388608 | tf_op jit(solution)/shard_map/all_to_all | solution.py:66
  1346.4 16.5 %copy.109 = bf16[16,8,64,4,64]{4,2,3,1,0:T(8,128)(2,1)} copy(bf16[16,8,64,4,64]{4,3,0,2,1:T(4,128)(2,1)} %bitcast.580) | data formatting | bytes 8388608 | tf_op jit(solution)/shard_map/all_to_all | solution.py:66
  1378.7 47.0 %fusion.318 = bf16[16,64,8192]{2,1,0:T(8,128)(2,1)} fusion(bf16[3,2048,8192]{2,1,0:T(8,128)(2,1)} %param.22, bf16[16,64,2048]{2,1,0:T(8,128)(2,1)} %get-tuple-element.268, f32[2048]{0:T(1024)S(1)} %bitcast.593, f32[16,64]{1,0:T(8,128)S(1)} %add_rsqrt_fusion), kind=kOutput, calls=%fused_computation.92.clone.clone.clone.clone.2 | convolution fusion | flops 34443624448 | bytes 54538240 | tf_op jit(solution)/shard_map/bsd,df->bsf/dot_general | solution.py:69
  1425.7 44.9 %fusion.155 = bf16[16,64,2048]{2,1,0:T(8,128)(2,1)} fusion(bf16[16,64,2048]{2,1,0:T(8,128)(2,1)} %get-tuple-element.268, bf16[3,8192,2048]{2,1,0:T(8,128)(2,1)} %param.23, bf16[16,64,8192]{2,1,0:T(8,128)(2,1)} %fusion.318), kind=kOutput, calls=%fused_computation.161 | convolution fusion | flops 34366029824 | bytes 58720256 | tf_op jit(solution)/shard_map/bsf,fd->bsd/dot_general | solution.py:70
  (192 shorter events, 737.5 us)
Async XLA Ops:
  5.4 53.4 %copy-start.10 = (f32[64,32]{0,1:T(8,128)}, f32[64,32]{0,1:T(8,128)S(1)}, u32[]{:S(2)}) copy-start(f32[64,32]{0,1:T(8,128)S(1)} %get-tuple-element.257) | copy-start | bytes 24580
  5.4 53.4 %copy-start.13 = (f32[64,32]{0,1:T(8,128)}, f32[64,32]{0,1:T(8,128)S(1)}, u32[]{:S(2)}) copy-start(f32[64,32]{0,1:T(8,128)S(1)} %get-tuple-element.258) | copy-start | bytes 24580
  16.4 37.9 %all-to-all-start.1 = ((bf16[8,2,32768]{2,1,0:T(2,128)(2,1)}), bf16[8,2,32768]{2,1,0:T(2,128)(2,1)S(1)}, u32[]{:S(2)}, u32[]{:S(2)}) async-start(bf16[8,2,32768]{2,1,0:T(2,128)(2,1)} %reshape.278), calls=%async_computation.1 | async-start | bytes 2097152 | tf_op jit(solution)/shard_map/all_to_all | solution.py:60
  21.8 23.4 %copy-start.5 = (bf16[16,64,2048]{2,1,0:T(8,128)(2,1)S(1)}, bf16[16,64,2048]{2,1,0:T(8,128)(2,1)}, u32[]{:S(2)}) copy-start(bf16[16,64,2048]{2,1,0:T(8,128)(2,1)} %param.16) | copy-start | bytes 12582916
  54.2 27.1 %all-to-all-start.2 = ((bf16[8,2,32768]{2,1,0:T(2,128)(2,1)}), bf16[8,2,32768]{2,1,0:T(2,128)(2,1)S(1)}, u32[]{:S(2)}, u32[]{:S(2)}) async-start(bf16[8,2,32768]{2,1,0:T(2,128)(2,1)} %reshape.280), calls=%async_computation.2 | async-start | bytes 2097152 | tf_op jit(solution)/shard_map/all_to_all | solution.py:61
  81.3 53.6 %all-to-all-start = ((bf16[8,2,131072]{2,1,0:T(2,128)(2,1)}), bf16[8,2,131072]{2,1,0:T(2,128)(2,1)}, u32[]{:S(2)}, u32[]{:S(2)}) async-start(bf16[8,2,131072]{2,1,0:T(2,128)(2,1)} %reshape.276), calls=%async_computation | async-start | bytes 8388608 | tf_op jit(solution)/shard_map/all_to_all | solution.py:59
  169.4 14.4 copy-start.9
  291.6 15.5 %copy-start.16 = (f32[3,2048]{1,0:T(4,128)S(1)}, f32[3,2048]{1,0:T(4,128)}, u32[]{:S(2)}) copy-start(f32[3,2048]{1,0:T(4,128)} %param.25) | copy-start | bytes 73732
  302.1 54.0 %all-to-all-start.3 = ((bf16[8,2,131072]{2,1,0:T(2,128)(2,1)}), bf16[8,2,131072]{2,1,0:T(2,128)(2,1)}, u32[]{:S(2)}, u32[]{:S(2)}) async-start(bf16[8,2,131072]{2,1,0:T(2,128)(2,1)} %reshape.282), calls=%async_computation.3 | async-start | bytes 8388608 | tf_op jit(solution)/shard_map/all_to_all | solution.py:66
  366.5 16.5 %copy-start.6 = (bf16[16,64,2048]{2,1,0:T(8,128)(2,1)S(1)}, bf16[16,64,2048]{2,1,0:T(8,128)(2,1)}, u32[]{:S(2)}) copy-start(bf16[16,64,2048]{2,1,0:T(8,128)(2,1)} %param.16) | copy-start | bytes 12582916
  445.6 45.4 %copy-start.19 = (f32[1,2048]{1,0:T(1,128)S(1)}, f32[1,2048]{1,0:T(1,128)}, u32[]{:S(2)}) copy-start(f32[1,2048]{1,0:T(1,128)} %get-tuple-element.256) | copy-start | bytes 24580
  527.0 18.9 %all-to-all-start.6 = ((bf16[8,2,32768]{2,1,0:T(2,128)(2,1)}), bf16[8,2,32768]{2,1,0:T(2,128)(2,1)S(1)}, u32[]{:S(2)}, u32[]{:S(2)}) async-start(bf16[8,2,32768]{2,1,0:T(2,128)(2,1)} %reshape.288), calls=%async_computation.6 | async-start | bytes 2097152 | tf_op jit(solution)/shard_map/all_to_all | solution.py:61
  545.9 26.1 %all-to-all-start.5 = ((bf16[8,2,32768]{2,1,0:T(2,128)(2,1)}), bf16[8,2,32768]{2,1,0:T(2,128)(2,1)S(1)}, u32[]{:S(2)}, u32[]{:S(2)}) async-start(bf16[8,2,32768]{2,1,0:T(2,128)(2,1)} %reshape.286), calls=%async_computation.5 | async-start | bytes 2097152 | tf_op jit(solution)/shard_map/all_to_all | solution.py:60
  572.0 53.6 %all-to-all-start.4 = ((bf16[8,2,131072]{2,1,0:T(2,128)(2,1)}), bf16[8,2,131072]{2,1,0:T(2,128)(2,1)}, u32[]{:S(2)}, u32[]{:S(2)}) async-start(bf16[8,2,131072]{2,1,0:T(2,128)(2,1)} %reshape.284), calls=%async_computation.4 | async-start | bytes 8388608 | tf_op jit(solution)/shard_map/all_to_all | solution.py:59
  659.8 14.4 copy-start.8
  856.4 16.5 %copy-start.24 = (bf16[16,64,2048]{2,1,0:T(8,128)(2,1)S(1)}, bf16[16,64,2048]{2,1,0:T(8,128)(2,1)}, u32[]{:S(2)}) copy-start(bf16[16,64,2048]{2,1,0:T(8,128)(2,1)} %get-tuple-element.262) | copy-start | bytes 12582916
  872.9 15.6 %copy-start.20 = (f32[1,2048]{1,0:T(1,128)S(1)}, f32[1,2048]{1,0:T(1,128)}, u32[]{:S(2)}) copy-start(f32[1,2048]{1,0:T(1,128)} %get-tuple-element.253) | copy-start | bytes 24580
  935.5 45.6 %copy-start.17 = (f32[1,2048]{1,0:T(1,128)S(1)}, f32[1,2048]{1,0:T(1,128)}, u32[]{:S(2)}) copy-start(f32[1,2048]{1,0:T(1,128)} %get-tuple-element.254) | copy-start | bytes 24580
  1017.0 18.9 %all-to-all-start.10 = ((bf16[8,2,32768]{2,1,0:T(2,128)(2,1)}), bf16[8,2,32768]{2,1,0:T(2,128)(2,1)S(1)}, u32[]{:S(2)}, u32[]{:S(2)}) async-start(bf16[8,2,32768]{2,1,0:T(2,128)(2,1)} %reshape.296), calls=%async_computation.10 | async-start | bytes 2097152 | tf_op jit(solution)/shard_map/all_to_all | solution.py:61
  1035.8 26.1 %all-to-all-start.9 = ((bf16[8,2,32768]{2,1,0:T(2,128)(2,1)}), bf16[8,2,32768]{2,1,0:T(2,128)(2,1)S(1)}, u32[]{:S(2)}, u32[]{:S(2)}) async-start(bf16[8,2,32768]{2,1,0:T(2,128)(2,1)} %reshape.294), calls=%async_computation.9 | async-start | bytes 2097152 | tf_op jit(solution)/shard_map/all_to_all | solution.py:60
  1061.9 53.6 %all-to-all-start.8 = ((bf16[8,2,131072]{2,1,0:T(2,128)(2,1)}), bf16[8,2,131072]{2,1,0:T(2,128)(2,1)}, u32[]{:S(2)}, u32[]{:S(2)}) async-start(bf16[8,2,131072]{2,1,0:T(2,128)(2,1)} %reshape.292), calls=%async_computation.8 | async-start | bytes 8388608 | tf_op jit(solution)/shard_map/all_to_all | solution.py:59
  1149.9 14.4 copy-start.7
  1346.4 16.5 %copy-start.23 = (bf16[16,64,2048]{2,1,0:T(8,128)(2,1)S(1)}, bf16[16,64,2048]{2,1,0:T(8,128)(2,1)}, u32[]{:S(2)}) copy-start(bf16[16,64,2048]{2,1,0:T(8,128)(2,1)} %get-tuple-element.266) | copy-start | bytes 12582916
  1362.9 15.8 %copy-start.18 = (f32[1,2048]{1,0:T(1,128)S(1)}, f32[1,2048]{1,0:T(1,128)}, u32[]{:S(2)}) copy-start(f32[1,2048]{1,0:T(1,128)} %get-tuple-element.251) | copy-start | bytes 24580
  (11 other events, 76.4 us)
where the time goes:
time: 1480 us; the launch traced here: 1470 us
  matrix products  618 us (42%)
  local copies, waits for them, and re-layouts  400 us (27%)
  waiting for transfers between devices  163 us (11%)
  other arithmetic  134 us (9%)
  blocking collectives  107 us (7%)
  starting transfers between devices  43.1 us (3%)
    unnamed x74, local copies, waits for them, and re-layouts  159 us
    dot_general x3, matrix products, layer_step(): jnp.einsum('bsd,df->bsf', normed_mlp, w_up, preferred_element_type=jnp.fl...  141 us
    dot_general x3, matrix products, layer_step(): jnp.einsum('bsf,fd->bsd', gelu_act, w_down, preferred_element_type=jnp.fl...  136 us
    all_to_all x2, blocking collectives, layer_step(): attn_loc = lax.all_to_all(attn_heads, 'seq', 1, 2, tiled=True)  107 us
    all_to_all x3, waiting for transfers between devices, layer_step(): q_all = lax.all_to_all(q_loc, 'seq', 2, 1, tiled=True)  106 us
    dot_general x6, matrix products, one_block(): jnp.einsum('bqkgd,bskd->bkgqs', q_blk, k_heads, preferred_element_type=jn...  94.7 us
    reduce_sum x6, other arithmetic, one_block(): row_sum = jnp.sum(exp_f32, axis=-1)  89.4 us
    dot_general x6, matrix products, one_block(): jnp.einsum('bkgqs,bskd->bqkgd', exp_f32.astype(jnp.bfloat16), v_heads, pr...  88.7 us
  transfers between devices with their start and end apart: 10, of which 6 were waited for; matrix products, arithmetic and copies ran while one was open for 10% of the time, Pallas kernels for 0%

commit v1 on v0

v1 whole, which is shorter than its diff:
```python
import functools

import jax
import jax.numpy as jnp
from jax import lax
from jax.experimental import pallas as pl
from jax.experimental.pallas import tpu as pltpu
from jax.sharding import PartitionSpec as P

ROPE_BASE = 10000.0
NORM_EPS = 1e-6
N_CHUNKS = 2
BLK = 512
N_ROW_SLOTS = 5
N_UP_SLOTS = 3


def rope_tables(positions, head_dim):
    inv_freq = ROPE_BASE ** (-jnp.arange(head_dim // 2, dtype=jnp.float32) * (2.0 / head_dim))
    angles = positions.astype(jnp.float32)[..., None] * inv_freq
    return jnp.cos(angles), jnp.sin(angles)


def gelu(x):
    c = 0.7978845608028654
    return 0.5 * x * (1.0 + jnp.tanh(c * (x + 0.044715 * (x * x * x))))


def norm_rows(src_ref, gain, dst_ref, rows, step=64):
    def body(i, _):
        sl = pl.ds(pl.multiple_of(i * step, step), step)
        x = src_ref[sl, :].astype(jnp.float32)
        ms = jnp.mean(x * x, axis=-1, keepdims=True)
        dst_ref[sl, :] = (x * lax.rsqrt(ms + NORM_EPS) * gain).astype(jnp.bfloat16)
        return 0

    lax.fori_loop(0, rows // step, body, 0)


def dense_kernel(layer, with_mlp, with_qkv, rows, seq_loc, d_model, ff_dim, x_row, y_row, aliased, *refs):
    it = iter(refs)
    x_hbm = next(it)
    if with_mlp:
        o_hbm, wo_hbm, wu_hbm, wd_hbm, gm_ref = (next(it) for _ in range(5))
    if with_qkv:
        wq_hbm, wk_hbm, wv_hbm, ga_ref, tab_ref = (next(it) for _ in range(5))
    if aliased:
        next(it)
    if with_mlp:
        y_hbm = next(it)
    if with_qkv:
        q_hbm, kv_hbm = next(it), next(it)
    x_ref, n_ref, ring, ring_sem, x_sem, out_sem = (next(it) for _ in range(6))
    if with_mlp:
        o_ref, acc_ref, a_ref, up_ring, up_sem, o_sem = (next(it) for _ in range(6))
    if with_qkv:
        st_ref = next(it)

    n_o = d_model // BLK
    n_f = ff_dim // BLK
    n_q = d_model // BLK
    o_base = 0
    f_base = n_o if with_mlp else 0
    q_base = f_base + (n_f if with_mlp else 0)
    mlp_layer = layer - 1

    def start_o(j, slot):
        for i in range(4):
            for par in range(2):
                pltpu.make_async_copy(
                    wo_hbm.at[mlp_layer, j * 8 + par * 4 + i],
                    ring.at[slot, pl.ds((i * 2 + par) * 64, 64)],
                    ring_sem.at[slot],
                ).start()

    def start_down(f, slot):
        pltpu.make_async_copy(
            wd_hbm.at[mlp_layer, pl.ds(pl.multiple_of(f * BLK, BLK), BLK)], ring.at[slot], ring_sem.at[slot]
        ).start()

    def start_q(j, slot):
        for i in range(4):
            for half in range(2):
                for par in range(2):
                    pltpu.make_async_copy(
                        wq_hbm.at[layer, j * 8 + par * 4 + i, pl.ds(half * 32, 32)],
                        ring.at[slot, pl.ds(i * 128 + half * 64 + par * 32, 32)],
                        ring_sem.at[slot],
                    ).start()

    def start_k(slot):
        for gp in range(4):
            for half in range(2):
                for par in range(2):
                    pltpu.make_async_copy(
                        wk_hbm.at[layer, gp * 2 + par, pl.ds(half * 32, 32)],
                        ring.at[slot, pl.ds(gp * 128 + half * 64 + par * 32, 32)],
                        ring_sem.at[slot],
                    ).start()

    def start_v(slot):
        for g in range(8):
            pltpu.make_async_copy(wv_hbm.at[layer, g], ring.at[slot, pl.ds(g * 64, 64)], ring_sem.at[slot]).start()

    n_blocks = q_base + ((n_q + 2) if with_qkv else 0)

    def start_block(b):
        static = isinstance(b, int)
        slot = b % N_ROW_SLOTS if static else lax.rem(b, N_ROW_SLOTS)

        def guard(lo, hi, fn):
            if static:
                if lo <= b < hi:
                    fn()
            else:
                pl.when(jnp.logical_and(b >= lo, b < hi))(fn)

        if with_mlp:
            guard(o_base, f_base, lambda: start_o(b, slot))
            guard(f_base, q_base, lambda: start_down(b - f_base, slot))
        if with_qkv:
            guard(q_base, q_base + n_q, lambda: start_q(b - q_base, slot))
            guard(q_base + n_q, q_base + n_q + 1, lambda: start_k(slot))
            guard(q_base + n_q + 1, q_base + n_q + 2, lambda: start_v(slot))

    def wait_block(b):
        slot = b % N_ROW_SLOTS if isinstance(b, int) else lax.rem(b, N_ROW_SLOTS)
        pltpu.make_async_copy(ring.at[slot], ring.at[slot], ring_sem.at[slot]).wait()
        return slot

    def start_up(f):
        slot = f % N_UP_SLOTS if isinstance(f, int) else lax.rem(f, N_UP_SLOTS)
        pltpu.make_async_copy(
            wu_hbm.at[mlp_layer, :, pl.ds(pl.multiple_of(f * BLK, BLK), BLK)], up_ring.at[slot], up_sem.at[slot]
        ).start()

    def wait_up(f):
        slot = lax.rem(f, N_UP_SLOTS)
        pltpu.make_async_copy(up_ring.at[slot], up_ring.at[slot], up_sem.at[slot]).wait()
        return slot

    if with_mlp:
        for j in range(n_o):
            pltpu.make_async_copy(o_hbm.at[:, pl.ds(j * BLK, BLK)], o_ref.at[j], o_sem.at[j]).start()
            if j == 0:
                start_block(0)
    x_copy = pltpu.make_async_copy(x_hbm.at[pl.ds(x_row, rows)], x_ref, x_sem)
    x_copy.start()
    for b in range(1 if with_mlp else 0, N_ROW_SLOTS - 1):
        start_block(b)
    if with_mlp:
        for f in range(N_UP_SLOTS - 1):
            start_up(f)

    if with_mlp:
        def o_body(j, _):
            pltpu.make_async_copy(o_ref.at[j], o_ref.at[j], o_sem.at[j]).wait()
            slot = wait_block(j)
            start_block(j + N_ROW_SLOTS - 1)
            part = jnp.dot(o_ref[j], ring[slot], preferred_element_type=jnp.float32)

            @pl.when(j == 0)
            def _():
                acc_ref[...] = part

            @pl.when(j > 0)
            def _():
                acc_ref[...] += part

            return 0

        lax.fori_loop(0, n_o, o_body, 0)
        x_copy.wait()

        def resid_body(i, _):
            sl = pl.ds(pl.multiple_of(i * 64, 64), 64)
            h = (x_ref[sl, :].astype(jnp.float32) + acc_ref[sl, :]).astype(jnp.bfloat16)
            hf = h.astype(jnp.float32)
            ms = jnp.mean(hf * hf, axis=-1, keepdims=True)
            n_ref[sl, :] = (hf * lax.rsqrt(ms + NORM_EPS) * gm_ref[0]).astype(jnp.bfloat16)
            acc_ref[sl, :] = hf
            return 0

        lax.fori_loop(0, rows // 64, resid_body, 0)

        def up_part(f):
            slot = wait_up(f)

            @pl.when(f + N_UP_SLOTS - 1 < n_f)
            def _():
                start_up(f + N_UP_SLOTS - 1)

            u = jnp.dot(n_ref[...], up_ring[slot], preferred_element_type=jnp.float32)
            a_ref[lax.rem(f, 2)] = gelu(u).astype(jnp.bfloat16)

        def down_part(f):
            b = f_base + f
            slot = wait_block(b)
            start_block(b + N_ROW_SLOTS - 1)
            acc_ref[...] += jnp.dot(a_ref[lax.rem(f, 2)], ring[slot], preferred_element_type=jnp.float32)

        def f_body(f, _):
            up_part(f)
            down_part(f)
            return 0

        lax.fori_loop(0, n_f, f_body, 0)

        def y_body(i, _):
            sl = pl.ds(pl.multiple_of(i * 64, 64), 64)
            y = acc_ref[sl, :].astype(jnp.bfloat16)
            x_ref[sl, :] = y
            if with_qkv:
                yf = y.astype(jnp.float32)
                ms = jnp.mean(yf * yf, axis=-1, keepdims=True)
                n_ref[sl, :] = (yf * lax.rsqrt(ms + NORM_EPS) * ga_ref[0]).astype(jnp.bfloat16)
            return 0

        lax.fori_loop(0, rows // 64, y_body, 0)
        y_copy = pltpu.make_async_copy(x_ref, y_hbm.at[pl.ds(y_row, rows)], out_sem.at[0])
        y_copy.start()
    else:
        x_copy.wait()
        norm_rows(x_ref, ga_ref[0], n_ref, rows)

    if with_qkv:
        reps = rows // seq_loc

        def project(b):
            slot = wait_block(b)
            start_block(b + N_ROW_SLOTS - 1)
            return lax.dot_general(n_ref[...], ring[slot], (((1,), (1,)), ((), ())), preferred_element_type=jnp.float32)

        def rope(t, cos_t, sin_t):
            r3 = t.reshape(reps, seq_loc, 128)
            s3 = pltpu.roll(t, 64, 1).reshape(reps, seq_loc, 128)
            return (r3 * cos_t + s3 * sin_t).reshape(rows, 128).astype(jnp.bfloat16)

        def drain(s, dst):
            pltpu.make_async_copy(st_ref.at[s], dst, out_sem.at[1 + s]).wait()

        def q_body(j, _):
            s = lax.rem(j, 2)
            res = project(q_base + j)

            @pl.when(j >= 2)
            def _():
                drain(s, q_hbm.at[:, pl.ds(0, BLK)])

            for i in range(4):
                st_ref[s, :, i * 128 : (i + 1) * 128] = rope(res[:, i * 128 : (i + 1) * 128], tab_ref[0], tab_ref[1])
            pltpu.make_async_copy(
                st_ref.at[s], q_hbm.at[:, pl.ds(pl.multiple_of(j * BLK, BLK), BLK)], out_sem.at[1 + s]
            ).start()
            return 0

        lax.fori_loop(0, n_q, q_body, 0)
        kres = project(q_base + n_q)
        drain(0, q_hbm.at[:, pl.ds(0, BLK)])
        for i in range(4):
            st_ref[0, :, i * 128 : (i + 1) * 128] = rope(kres[:, i * 128 : (i + 1) * 128], tab_ref[2], tab_ref[3])
        pltpu.make_async_copy(st_ref.at[0], kv_hbm.at[:, pl.ds(0, BLK)], out_sem.at[1]).start()
        vres = project(q_base + n_q + 1)
        drain(1, q_hbm.at[:, pl.ds(0, BLK)])
        st_ref[1] = vres.astype(jnp.bfloat16)
        pltpu.make_async_copy(st_ref.at[1], kv_hbm.at[:, pl.ds(BLK, BLK)], out_sem.at[2]).start()
        drain(0, kv_hbm.at[:, pl.ds(0, BLK)])
        drain(1, kv_hbm.at[:, pl.ds(BLK, BLK)])
    if with_mlp:
        y_copy.wait()


def dense_call(layer, n_layers, x, x_row, rows, o, weights, tables, seq_loc, y_rows=None, y_row=0, y_into=None):
    w_query_t, w_key_t, w_value_t, w_out, w_up, w_down, g_attn, g_mlp = weights
    d_model = x.shape[1]
    ff_dim = w_up.shape[2]
    with_mlp = o is not None
    with_qkv = layer < n_layers
    any_spec = pl.BlockSpec(memory_space=pl.ANY)
    vmem_spec = pl.BlockSpec(memory_space=pltpu.VMEM)
    args, specs = [x], [any_spec]
    outs, out_specs = [], []
    flops = 0
    nbytes = 0
    if with_mlp:
        args += [o, w_out, w_up, w_down, g_mlp[layer - 1][None]]
        specs += [any_spec] * 4 + [vmem_spec]
        outs.append(jax.ShapeDtypeStruct((y_rows or rows, d_model), jnp.bfloat16))
        flops += 2 * rows * d_model * (d_model + 2 * ff_dim)
        nbytes += 2 * d_model * (d_model + 2 * ff_dim) + 6 * rows * d_model
    if with_qkv:
        args += [w_query_t, w_key_t, w_value_t, g_attn[layer][None], tables]
        specs += [any_spec] * 3 + [vmem_spec] * 2
        outs.append(jax.ShapeDtypeStruct((rows, d_model), jnp.bfloat16))
        outs.append(jax.ShapeDtypeStruct((rows, 2 * BLK), jnp.bfloat16))
        flops += 2 * rows * d_model * (d_model + 2 * BLK)
        nbytes += 2 * d_model * (d_model + 2 * BLK) + 5 * rows * d_model
    aliases = {}
    if y_into is not None:
        aliases = {len(args): 0}
        args.append(y_into)
        specs.append(any_spec)
    out_specs = [any_spec] * len(outs)
    scratch = [
        pltpu.VMEM((rows, d_model), jnp.bfloat16),
        pltpu.VMEM((rows, d_model), jnp.bfloat16),
        pltpu.VMEM((N_ROW_SLOTS, BLK, d_model), jnp.bfloat16),
        pltpu.SemaphoreType.DMA((N_ROW_SLOTS,)),
        pltpu.SemaphoreType.DMA,
        pltpu.SemaphoreType.DMA((3,)),
    ]
    if with_mlp:
        scratch += [
            pltpu.VMEM((d_model // BLK, rows, BLK), jnp.bfloat16),
            pltpu.VMEM((rows, d_model), jnp.float32),
            pltpu.VMEM((2, rows, BLK), jnp.bfloat16),
            pltpu.VMEM((N_UP_SLOTS, d_model, BLK), jnp.bfloat16),
            pltpu.SemaphoreType.DMA((N_UP_SLOTS,)),
            pltpu.SemaphoreType.DMA((d_model // BLK,)),
        ]
    if with_qkv:
        scratch.append(pltpu.VMEM((2, rows, BLK), jnp.bfloat16))
    return pl.pallas_call(
        functools.partial(
            dense_kernel, layer, with_mlp, with_qkv, rows, seq_loc, d_model, ff_dim, x_row, y_row, y_into is not None
        ),
        out_shape=outs,
        in_specs=specs,
        out_specs=out_specs,
        scratch_shapes=scratch,
        input_output_aliases=aliases,
        compiler_params=pltpu.CompilerParams(vmem_limit_bytes=60 * 1024 * 1024),
        cost_estimate=pl.CostEstimate(flops=flops, bytes_accessed=nbytes, transcendentals=0),
        name=f"dense_{int(with_mlp)}{int(with_qkv)}",
    )(*args)


def attn_kernel(n_dev, seq_loc, q_ref, kv_ref, bias_ref, o_ref):
    keys = n_dev * seq_loc
    lane = lax.broadcasted_iota(jnp.int32, (1, 128), 1)
    even = lax.rem(lane, 64) < 32
    first = lane < 64
    zero = jnp.zeros((), jnp.bfloat16)
    for gp in range(4):
        k_t = kv_ref[:, 0, :, gp * 128 : (gp + 1) * 128].reshape(keys, 128)
        v_t = kv_ref[:, 0, :, BLK + gp * 128 : BLK + (gp + 1) * 128].reshape(keys, 128)
        q_rows = []
        for i in range(4):
            c0 = gp * BLK + i * 128
            q_t = q_ref[0, :, c0 : c0 + 128]
            q_rows += [jnp.where(even, q_t, zero), jnp.where(even, zero, q_t)]
        q_s = jnp.concatenate(q_rows, axis=0)
        s = lax.dot_general(q_s, k_t, (((1,), (1,)), ((), ())), preferred_element_type=jnp.float32)
        s = (s.reshape(8, seq_loc, keys) + bias_ref[...][None]).reshape(8 * seq_loc, keys)
        m = jnp.max(s, axis=-1, keepdims=True)
        p = jnp.exp(s - m)
        l = jnp.sum(p, axis=-1, keepdims=True)
        acc = jnp.dot(p.astype(jnp.bfloat16), v_t, preferred_element_type=jnp.float32)
        o = (acc / l).reshape(4, 2, seq_loc, 128)
        for i in range(4):
            c0 = gp * BLK + i * 128
            o_ref[0, :, c0 : c0 + 128] = jnp.where(first, o[i, 0], o[i, 1]).astype(jnp.bfloat16)


def attn_call(q, kv, bias, seq_loc):
    rows, d_model = q.shape
    n_dev = kv.shape[0]
    n_b = rows // seq_loc
    keys = n_dev * seq_loc
    out = pl.pallas_call(
        functools.partial(attn_kernel, n_dev, seq_loc),
        grid=(n_b,),
        out_shape=jax.ShapeDtypeStruct((n_b, seq_loc, d_model), jnp.bfloat16),
        in_specs=[
            pl.BlockSpec((1, seq_loc, d_model), lambda b: (b, 0, 0)),
            pl.BlockSpec((n_dev, 1, seq_loc, 2 * BLK), lambda b: (0, b, 0, 0)),
            pl.BlockSpec((seq_loc, keys), lambda b: (0, 0)),
        ],
        out_specs=pl.BlockSpec((1, seq_loc, d_model), lambda b: (b, 0, 0)),
        compiler_params=pltpu.CompilerParams(
            dimension_semantics=("arbitrary",), vmem_limit_bytes=60 * 1024 * 1024
        ),
        cost_estimate=pl.CostEstimate(
            flops=16 * rows * d_model * keys, bytes_accessed=2 * kv.size + 4 * q.size, transcendentals=0
        ),
        name="attn",
    )(q.reshape(n_b, seq_loc, d_model), kv.reshape(n_dev, n_b, seq_loc, 2 * BLK), bias)
    return out.reshape(rows, d_model)


def solution(mesh):
    tok_spec = P(None, ("data", "seq"), None)
    in_specs = (tok_spec, P(("data", "seq"))) + (P(),) * 8

    def device_fn(x_loc, pos_loc, w_query, w_key, w_value, w_out, w_up, w_down, g_attn, g_mlp):
        n_batch, seq_loc, d_model = x_loc.shape
        n_layers = w_query.shape[0]
        n_dev = mesh.shape["seq"]
        scale = w_query.shape[-1] ** -0.5
        cos_t, sin_t = rope_tables(pos_loc, w_query.shape[-1])
        cos4 = jnp.concatenate([cos_t] * 4, axis=-1)
        sin4 = jnp.concatenate([-sin_t, -sin_t, sin_t, sin_t], axis=-1)
        tables = jnp.stack([cos4 * scale, sin4 * scale, cos4, sin4])
        me = lax.axis_index("seq")
        key_pos = jnp.arange(n_dev * seq_loc)
        query_pos = me * seq_loc + jnp.arange(seq_loc)
        bias = jnp.where(key_pos[None, :] <= query_pos[:, None], 0.0, -jnp.inf).astype(jnp.float32)
        weights = (
            jnp.transpose(w_query, (0, 2, 3, 1)),
            jnp.transpose(w_key, (0, 2, 3, 1)),
            jnp.transpose(w_value, (0, 2, 3, 1)),
            w_out,
            w_up,
            w_down,
            g_attn,
            g_mlp,
        )
        rows = n_batch // N_CHUNKS * seq_loc
        x_all = x_loc.reshape(n_batch * seq_loc, d_model)
        xs = [(x_all, c * rows) for c in range(N_CHUNKS)]
        qs, kvs = [None] * N_CHUNKS, [None] * N_CHUNKS
        for c in range(N_CHUNKS):
            qs[c], kv = dense_call(0, n_layers, *xs[c], rows, None, weights, tables, seq_loc)
            kvs[c] = lax.all_gather(kv, "seq", axis=0, tiled=False)
        out = None
        last = None
        for layer in range(1, n_layers + 1):
            for c in range(N_CHUNKS):
                if last is not None:
                    qs[c], _ = lax.optimization_barrier((qs[c], last))
                o = attn_call(qs[c], kvs[c], bias, seq_loc)
                if layer < n_layers:
                    y, qs[c], kv = dense_call(layer, n_layers, *xs[c], rows, o, weights, tables, seq_loc)
                    xs[c] = (y, 0)
                    kvs[c] = lax.all_gather(kv, "seq", axis=0, tiled=False)
                    last = y
                else:
                    (out,) = dense_call(
                        layer, n_layers, *xs[c], rows, o, weights, tables, seq_loc, n_batch * seq_loc, c * rows, out
                    )
                    last = out
        return out.reshape(n_batch, seq_loc, d_model)

    return jax.shard_map(device_fn, mesh=mesh, in_specs=in_specs, out_specs=tok_spec, check_vma=False)
```

time: 1480 us -> 579 us (0.39)
  matrix products: 618 us -> 0 us
  Pallas kernels: 0 us -> 518 us
  local copies, waits for them, and re-layouts: 400 us -> 2.12 us
  other arithmetic: 134 us -> 2.49 us
  waiting for transfers between devices: 163 us -> 34.7 us
  blocking collectives: 107 us -> 0 us
  starting transfers between devices: 43.1 us -> 1.17 us
    dot_general x30 -> x0, matrix products: 618 us -> none  [the longest x3 141 us: layer_step(): jnp.einsum('bsd,df->bsf', normed_mlp, w_up, preferred_element_type=jnp.fl...]
    pallas_call x0 -> x14, Pallas kernels: none -> 518 us  [the longest x8 425 us: dense_call(): pl.pallas_call(functools.partial(dense_kernel, layer, with_mlp, with_qkv,...]
    all_to_all x10 -> x0, waiting for transfers between devices: 163 us -> none  [the longest x3 106 us: layer_step(): q_all = lax.all_to_all(q_loc, 'seq', 2, 1, tiled=True)]
    unnamed x74 -> x2, local copies, waits for them, and re-layouts: 159 us -> 0.01 us
    all_to_all x24 -> x0, local copies, waits for them, and re-layouts: 151 us -> none  [the longest x3 71 us: layer_step(): q_all = lax.all_to_all(q_loc, 'seq', 2, 1, tiled=True)]
    all_to_all x2 -> x0, blocking collectives: 107 us -> none  [layer_step(): attn_loc = lax.all_to_all(attn_heads, 'seq', 1, 2, tiled=True)]
    reduce_sum x7 -> x0, other arithmetic: 92.5 us -> none  [the longest x6 89.4 us: one_block(): row_sum = jnp.sum(exp_f32, axis=-1)]
    reshape x6 -> x0, local copies, waits for them, and re-layouts: 77 us -> none  [the longest x3 41.4 us: causal_attention(): jnp.moveaxis(blocks, 0, 1)]
  transfers between devices with their start and end apart: 10 -> 6, of which waited for: 6 -> 1; matrix products, arithmetic and copies ran while one was open for 10% -> 0% of each run, Pallas kernels for 0% -> 75%
where the time goes in v1:
time: 579 us; the launch traced here: 572 us
  Pallas kernels  518 us (89%)
  waiting for transfers between devices  34.7 us (6%)
  between operations  13.9 us (2%)
    pallas_call x8, Pallas kernels, dense_call(): pl.pallas_call(functools.partial(dense_kernel, layer, with_mlp, with_qkv,...  425 us
    pallas_call x6, Pallas kernels, attn_call(): pl.pallas_call(functools.partial(attn_kernel, n_dev, seq_loc), grid=(n_b,...  93.3 us
    all_gather x6, waiting for transfers between devices, device_fn(): kvs[c] = lax.all_gather(kv, 'seq', axis=0, tiled=False)  34.6 us
  transfers between devices with their start and end apart: 6, of which 1 were waited for; matrix products, arithmetic and copies ran while one was open for 0% of the time, Pallas kernels for 75%

profile of v1, /device:TPU:0, one launch (start us, length us, event | category | flops | bytes accessed | tf_op | source)
XLA Modules:
  0.0 572.2 jit_solution(5526303659088282540)
XLA Ops:
  6.5 0.7 convert_element_type.3
  7.2 1.5 fusion.6
  9.2 0.7 pad_maximum_fusion.refs_5_.refs_10_
  9.8 16.9 %dense_01.3 = (bf16[512,2048]{1,0:T(8,128)(2,1)}, bf16[512,1024]{1,0:T(8,128)(2,1)}) custom-call(bf16[1024,2048]{1,0:T(8,128)(2,1)} %bitcast.51, bf16[3,32,64,2048]{3,2,1,0:T(8,128)(2,1)} %bitcast.33, bf16[3,8,64,2048]{3,2,1,0:T(8,128)(2,1)} %bitcast.39, bf16[3,8,64,2048]{3,2,1,0:T(8,128)(2,1)} %bitcast.45, f32[1,2048]{1,0:T(1,128)} %get-tuple-element.51.refs_4_, ...), custom_call_target="tpu_custom_call" | custom-call | flops 6442450944 | bytes 17825792 | tf_op jit(solution)/shard_map/dense_01/pallas_call | solution.py:323
  26.8 17.0 %dense_01.2 = (bf16[512,2048]{1,0:T(8,128)(2,1)}, bf16[512,1024]{1,0:T(8,128)(2,1)}) custom-call(bf16[1024,2048]{1,0:T(8,128)(2,1)} %bitcast.52, bf16[3,32,64,2048]{3,2,1,0:T(8,128)(2,1)} %bitcast.34, bf16[3,8,64,2048]{3,2,1,0:T(8,128)(2,1)} %bitcast.40, bf16[3,8,64,2048]{3,2,1,0:T(8,128)(2,1)} %bitcast.46, f32[1,2048]{1,0:T(1,128)} %get-tuple-element.51.refs_4_, ...), custom_call_target="tpu_custom_call" | custom-call | flops 6442450944 | bytes 17825792 | tf_op jit(solution)/shard_map/dense_01/pallas_call | solution.py:323
  43.8 0.2 all-gather.17.cloned.1.call-start
  44.1 0.7 fusion.bias_ref
  44.8 0.6 fusion.5
  45.4 34.5 %all-gather.13.cloned.1.call-done = bf16[4096,1024]{1,0:T(8,128)(2,1)} async-done(((bf16[512,1024]{1,0:T(8,128)(2,1)}), bf16[4096,1024]{1,0:T(8,128)(2,1)}) %all-gather.13.cloned.1.call-update) | async-done | bytes 8388624 | tf_op jit(solution)/shard_map/all_gather | solution.py:424
  79.9 15.5 %attn.6 = bf16[8,64,2048]{2,1,0:T(8,128)(2,1)} custom-call(bf16[8,64,2048]{2,1,0:T(8,128)(2,1)} %bitcast.68, bf16[8,8,64,1024]{3,2,1,0:T(8,128)(2,1)} %bitcast.62, f32[64,512]{1,0:T(8,128)} %fusion.bias_ref), custom_call_target="tpu_custom_call" | custom-call | flops 8589934592 | bytes 12582912 | tf_op jit(solution)/shard_map/attn/pallas_call | solution.py:370
  95.4 69.0 %dense_11.4 = (bf16[512,2048]{1,0:T(8,128)(2,1)}, bf16[512,2048]{1,0:T(8,128)(2,1)}, bf16[512,1024]{1,0:T(8,128)(2,1)}) custom-call(bf16[1024,2048]{1,0:T(8,128)(2,1)} %bitcast.53, bf16[512,2048]{1,0:T(8,128)(2,1)} %bitcast.59, bf16[3,32,64,2048]{3,2,1,0:T(8,128)(2,1)} %refs_2_.11, bf16[3,2048,8192]{2,1,0:T(8,128)(2,1)} %refs_3_.11, ...), custom_call_target="tpu_custom_call" | custom-call | flops 45097156608 | bytes 99614720 | tf_op jit(solution)/shard_map/dense_11/pallas_call | solution.py:323
  164.5 0.3 all-gather.19.cloned.1.call-start
  164.8 15.6 %attn.7 = bf16[8,64,2048]{2,1,0:T(8,128)(2,1)} custom-call(bf16[8,64,2048]{2,1,0:T(8,128)(2,1)} %bitcast.67, bf16[8,8,64,1024]{3,2,1,0:T(8,128)(2,1)} %bitcast.61, f32[64,512]{1,0:T(8,128)} %fusion.bias_ref), custom_call_target="tpu_custom_call" | custom-call | flops 8589934592 | bytes 12582912 | tf_op jit(solution)/shard_map/attn/pallas_call | solution.py:370
  180.3 68.9 %dense_11.5 = (bf16[512,2048]{1,0:T(8,128)(2,1)}, bf16[512,2048]{1,0:T(8,128)(2,1)}, bf16[512,1024]{1,0:T(8,128)(2,1)}) custom-call(bf16[1024,2048]{1,0:T(8,128)(2,1)} %bitcast.54, bf16[512,2048]{1,0:T(8,128)(2,1)} %bitcast.56, bf16[3,32,64,2048]{3,2,1,0:T(8,128)(2,1)} %refs_2_.11, bf16[3,2048,8192]{2,1,0:T(8,128)(2,1)} %refs_3_.11, ...), custom_call_target="tpu_custom_call" | custom-call | flops 45097156608 | bytes 99614720 | tf_op jit(solution)/shard_map/dense_11/pallas_call | solution.py:323
  249.3 0.4 all-gather.21.cloned.1.call-start
  249.8 15.5 %attn.8 = bf16[8,64,2048]{2,1,0:T(8,128)(2,1)} custom-call(bf16[8,64,2048]{2,1,0:T(8,128)(2,1)} %bitcast.71, bf16[8,8,64,1024]{3,2,1,0:T(8,128)(2,1)} %bitcast.63, f32[64,512]{1,0:T(8,128)} %fusion.bias_ref), custom_call_target="tpu_custom_call" | custom-call | flops 8589934592 | bytes 12582912 | tf_op jit(solution)/shard_map/attn/pallas_call | solution.py:370
  265.3 69.0 %dense_11.6 = (bf16[512,2048]{1,0:T(8,128)(2,1)}, bf16[512,2048]{1,0:T(8,128)(2,1)}, bf16[512,1024]{1,0:T(8,128)(2,1)}) custom-call(bf16[512,2048]{1,0:T(8,128)(2,1)} %get-tuple-element.29.refs_0_, bf16[512,2048]{1,0:T(8,128)(2,1)} %bitcast.57, bf16[3,32,64,2048]{3,2,1,0:T(8,128)(2,1)} %refs_2_.11, bf16[3,2048,8192]{2,1,0:T(8,128)(2,1)} %refs_3_.11, ...), custom_call_target="tpu_custom_call" | custom-call | flops 45097156608 | bytes 99614720 | tf_op jit(solution)/shard_map/dense_11/pallas_call | solution.py:323
  334.3 0.2 all-gather.23.cloned.1.call-start
  334.6 15.6 %attn.9 = bf16[8,64,2048]{2,1,0:T(8,128)(2,1)} custom-call(bf16[8,64,2048]{2,1,0:T(8,128)(2,1)} %bitcast.69, bf16[8,8,64,1024]{3,2,1,0:T(8,128)(2,1)} %bitcast.64, f32[64,512]{1,0:T(8,128)} %fusion.bias_ref), custom_call_target="tpu_custom_call" | custom-call | flops 8589934592 | bytes 12582912 | tf_op jit(solution)/shard_map/attn/pallas_call | solution.py:370
  350.1 68.9 %dense_11.7 = (bf16[512,2048]{1,0:T(8,128)(2,1)}, bf16[512,2048]{1,0:T(8,128)(2,1)}, bf16[512,1024]{1,0:T(8,128)(2,1)}) custom-call(bf16[512,2048]{1,0:T(8,128)(2,1)} %get-tuple-element.32.refs_0_, bf16[512,2048]{1,0:T(8,128)(2,1)} %bitcast.55, bf16[3,32,64,2048]{3,2,1,0:T(8,128)(2,1)} %refs_2_.11, bf16[3,2048,8192]{2,1,0:T(8,128)(2,1)} %refs_3_.11, ...), custom_call_target="tpu_custom_call" | custom-call | flops 45097156608 | bytes 99614720 | tf_op jit(solution)/shard_map/dense_11/pallas_call | solution.py:323
  419.1 15.6 %attn.10 = bf16[8,64,2048]{2,1,0:T(8,128)(2,1)} custom-call(bf16[8,64,2048]{2,1,0:T(8,128)(2,1)} %bitcast.70, bf16[8,8,64,1024]{3,2,1,0:T(8,128)(2,1)} %bitcast.65, f32[64,512]{1,0:T(8,128)} %fusion.bias_ref), custom_call_target="tpu_custom_call" | custom-call | flops 8589934592 | bytes 12582912 | tf_op jit(solution)/shard_map/attn/pallas_call | solution.py:370
  434.7 57.4 %dense_10.2.refs_6_ = bf16[1024,2048]{1,0:T(8,128)(2,1)} custom-call(bf16[512,2048]{1,0:T(8,128)(2,1)} %get-tuple-element.37.refs_0_, bf16[512,2048]{1,0:T(8,128)(2,1)} %bitcast.60, bf16[3,32,64,2048]{3,2,1,0:T(8,128)(2,1)} %refs_2_.11, bf16[3,2048,8192]{2,1,0:T(8,128)(2,1)} %refs_3_.11, bf16[3,8192,2048]{2,1,0:T(8,128)(2,1)} %refs_4_.11, ...), custom_call_target="tpu_custom_call" | custom-call | flops 38654705664 | bytes 81788928 | tf_op jit(solution)/shard_map/dense_10/pallas_call | solution.py:323
  492.2 15.5 %attn.11 = bf16[8,64,2048]{2,1,0:T(8,128)(2,1)} custom-call(bf16[8,64,2048]{2,1,0:T(8,128)(2,1)} %bitcast.72, bf16[8,8,64,1024]{3,2,1,0:T(8,128)(2,1)} %bitcast.66, f32[64,512]{1,0:T(8,128)} %fusion.bias_ref), custom_call_target="tpu_custom_call" | custom-call | flops 8589934592 | bytes 12582912 | tf_op jit(solution)/shard_map/attn/pallas_call | solution.py:370
  507.7 57.4 %dense_10.3 = bf16[1024,2048]{1,0:T(8,128)(2,1)} custom-call(bf16[512,2048]{1,0:T(8,128)(2,1)} %get-tuple-element.40.refs_0_, bf16[512,2048]{1,0:T(8,128)(2,1)} %bitcast.58, bf16[3,32,64,2048]{3,2,1,0:T(8,128)(2,1)} %refs_2_.11, bf16[3,2048,8192]{2,1,0:T(8,128)(2,1)} %refs_3_.11, bf16[3,8192,2048]{2,1,0:T(8,128)(2,1)} %refs_4_.11, ...), custom_call_target="tpu_custom_call", output_to_operand_aliasing={{}: (6, {})} | custom-call | flops 38654705664 | bytes 81788928 | tf_op jit(solution)/shard_map/dense_10/pallas_call | solution.py:323
  (20 shorter events, 0.7 us)
Async XLA Ops:
  6.5 73.4 %all-gather.13.cloned.1.call-start = ((), (), s32[]{:S(2)}) async-start(), calls=%async_computation | async-start | bytes 9437184 | tf_op jit(solution)/shard_map/all_gather | solution.py:424
  26.8 18.0 %copy-start = (f32[3,2048]{1,0:T(4,128)S(1)}, f32[3,2048]{1,0:T(4,128)}, u32[]{:S(2)}) copy-start(f32[3,2048]{1,0:T(4,128)} %param.19) | copy-start | bytes 73732
  26.8 138.0 %all-gather.15.cloned.1.call-start = ((), (), s32[]{:S(2)}) async-start(), calls=%async_computation.1 | async-start | bytes 9437184 | tf_op jit(solution)/shard_map/all_gather | solution.py:424
  43.8 206.0 %all-gather.17.cloned.1.call-start = ((), (), s32[]{:S(2)}) async-start(), calls=%async_computation.2 | async-start | bytes 9437184 | tf_op jit(solution)/shard_map/all_gather | solution.py:435
  164.5 170.1 %all-gather.19.cloned.1.call-start = ((), (), s32[]{:S(2)}) async-start(), calls=%async_computation.3 | async-start | bytes 9437184 | tf_op jit(solution)/shard_map/all_gather | solution.py:435
  249.3 169.8 %all-gather.21.cloned.1.call-start = ((), (), s32[]{:S(2)}) async-start(), calls=%async_computation.4 | async-start | bytes 9437184 | tf_op jit(solution)/shard_map/all_gather | solution.py:435
  334.3 157.8 %all-gather.23.cloned.1.call-start = ((), (), s32[]{:S(2)}) async-start(), calls=%async_computation.5 | async-start | bytes 9437184 | tf_op jit(solution)/shard_map/all_gather | solution.py:435
Sparse Core Ops, SparseCore 0:
  26.9 52.9 all-gather.12
  81.7 50.1 all-gather.14
  164.6 50.1 all-gather.16
  249.4 50.1 all-gather.18
  334.4 50.1 all-gather.20
  419.2 50.2 all-gather.22

commit v2 on v1

v2 whole, which is shorter than its diff:
```python
import functools

import jax
import jax.numpy as jnp
from jax import lax
from jax.experimental import pallas as pl
from jax.experimental.pallas import tpu as pltpu
from jax.sharding import PartitionSpec as P

ROPE_BASE = 10000.0
NORM_EPS = 1e-6
N_CHUNKS = 2
BLK = 512
N_ROW_SLOTS = 6
N_UP_SLOTS = 4
N_KV_SLOTS = 3
MASK_VALUE = -3.38e38


def rope_tables(positions, head_dim):
    inv_freq = ROPE_BASE ** (-jnp.arange(head_dim // 2, dtype=jnp.float32) * (2.0 / head_dim))
    angles = positions.astype(jnp.float32)[..., None] * inv_freq
    return jnp.cos(angles), jnp.sin(angles)


def gelu(x):
    c = 0.7978845608028654
    return 0.5 * x * (1.0 + jnp.tanh(c * (x + 0.044715 * (x * x * x))))


def norm_rows(src_ref, gain, dst_ref, rows, step=64):
    def body(i, _):
        sl = pl.ds(pl.multiple_of(i * step, step), step)
        x = src_ref[sl, :].astype(jnp.float32)
        ms = jnp.mean(x * x, axis=-1, keepdims=True)
        dst_ref[sl, :] = (x * lax.rsqrt(ms + NORM_EPS) * gain).astype(jnp.bfloat16)
        return 0

    lax.fori_loop(0, rows // step, body, 0)


def layer_kernel(layer, with_mlp, with_q, with_kv, rows, seq_loc, n_dev, d_model, ff_dim, x_row, y_row, aliased, *refs):
    with_qkv = with_q or with_kv
    it = iter(refs)
    x_hbm = next(it)
    if with_mlp:
        qin_hbm, kvin_hbm, mask_ref, wo_hbm, wu_hbm, wd_hbm, gm_ref = (next(it) for _ in range(7))
    if with_qkv:
        wq_hbm, wk_hbm, wv_hbm, ga_ref, tab_ref = (next(it) for _ in range(5))
    if aliased:
        next(it)
    if with_mlp:
        y_hbm = next(it)
    if with_q:
        q_hbm = next(it)
    if with_kv:
        kv_hbm = next(it)
    x_ref, n_ref, ring, ring_sem, x_sem, out_sem = (next(it) for _ in range(6))
    if with_mlp:
        o_ref, acc_ref, u_ref, a_ref, up_ring, up_sem, q_ref, q_sem, kv_ring, kv_sem = (next(it) for _ in range(10))
    if with_qkv:
        st_ref = next(it)

    n_o = d_model // BLK
    n_f = ff_dim // BLK
    n_q = d_model // BLK if with_q else 0
    n_kv = 2 if with_kv else 0
    o_base = 0
    f_base = n_o if with_mlp else 0
    q_base = f_base + (n_f if with_mlp else 0)
    mlp_layer = layer - 1

    def start_o(j, slot):
        for i in range(4):
            for par in range(2):
                pltpu.make_async_copy(
                    wo_hbm.at[mlp_layer, j * 8 + par * 4 + i],
                    ring.at[slot, pl.ds((i * 2 + par) * 64, 64)],
                    ring_sem.at[slot],
                ).start()

    def start_down(f, slot):
        for z in range(4):
            row = f * BLK + z * 128
            pltpu.make_async_copy(
                wd_hbm.at[mlp_layer, pl.ds(row if isinstance(f, int) else pl.multiple_of(row, 128), 128)],
                ring.at[slot, pl.ds(z * 128, 128)],
                ring_sem.at[slot],
            ).start()

    def start_q(j, slot):
        for i in range(4):
            for half in range(2):
                for par in range(2):
                    pltpu.make_async_copy(
                        wq_hbm.at[layer, j * 8 + par * 4 + i, pl.ds(half * 32, 32)],
                        ring.at[slot, pl.ds(i * 128 + half * 64 + par * 32, 32)],
                        ring_sem.at[slot],
                    ).start()

    def start_k(slot):
        for gp in range(4):
            for half in range(2):
                for par in range(2):
                    pltpu.make_async_copy(
                        wk_hbm.at[layer, gp * 2 + par, pl.ds(half * 32, 32)],
                        ring.at[slot, pl.ds(gp * 128 + half * 64 + par * 32, 32)],
                        ring_sem.at[slot],
                    ).start()

    def start_v(slot):
        for g in range(8):
            pltpu.make_async_copy(wv_hbm.at[layer, g], ring.at[slot, pl.ds(g * 64, 64)], ring_sem.at[slot]).start()

    n_blocks = q_base + n_q + n_kv

    def start_block(b):
        static = isinstance(b, int)
        slot = b % N_ROW_SLOTS if static else lax.rem(b, N_ROW_SLOTS)

        def guard(lo, hi, fn):
            if static:
                if lo <= b < hi:
                    fn()
            else:
                pl.when(jnp.logical_and(b >= lo, b < hi))(fn)

        if with_mlp:
            guard(o_base, f_base, lambda: start_o(b, slot))
            guard(f_base, q_base, lambda: start_down(b - f_base, slot))
        if with_q:
            guard(q_base, q_base + n_q, lambda: start_q(b - q_base, slot))
        if with_kv:
            guard(q_base + n_q, q_base + n_q + 1, lambda: start_k(slot))
            guard(q_base + n_q + 1, q_base + n_q + 2, lambda: start_v(slot))

    def wait_block(b):
        slot = b % N_ROW_SLOTS if isinstance(b, int) else lax.rem(b, N_ROW_SLOTS)
        pltpu.make_async_copy(ring.at[slot], ring.at[slot], ring_sem.at[slot]).wait()
        return slot

    def start_up(f):
        slot = f % N_UP_SLOTS if isinstance(f, int) else lax.rem(f, N_UP_SLOTS)
        col = f * BLK if isinstance(f, int) else pl.multiple_of(f * BLK, BLK)
        for z in range(4):
            pltpu.make_async_copy(
                wu_hbm.at[mlp_layer, pl.ds(z * BLK, BLK), pl.ds(col, BLK)],
                up_ring.at[slot, pl.ds(z * BLK, BLK)],
                up_sem.at[slot],
            ).start()

    def wait_up(f):
        slot = f % N_UP_SLOTS if isinstance(f, int) else lax.rem(f, N_UP_SLOTS)
        pltpu.make_async_copy(up_ring.at[slot], up_ring.at[slot], up_sem.at[slot]).wait()
        return slot

    n_b = rows // seq_loc

    def start_kv(i):
        slot = i % N_KV_SLOTS if isinstance(i, int) else lax.rem(i, N_KV_SLOTS)
        row = i * seq_loc if isinstance(i, int) else pl.multiple_of(i * seq_loc, seq_loc)
        pltpu.make_async_copy(kvin_hbm.at[:, pl.ds(row, seq_loc)], kv_ring.at[slot], kv_sem.at[slot]).start()

    x_copy = pltpu.make_async_copy(x_hbm.at[pl.ds(x_row, rows)], x_ref, x_sem)
    if with_mlp:
        q_copy = pltpu.make_async_copy(qin_hbm, q_ref, q_sem)
        q_copy.start()
        for i in range(N_KV_SLOTS - 1):
            start_kv(i)
    x_copy.start()
    for b in range(min(N_ROW_SLOTS - 1, n_blocks)):
        start_block(b)
    if with_mlp:
        for f in range(N_UP_SLOTS):
            start_up(f)

    if with_mlp:
        keys = n_dev * seq_loc
        lane = lax.broadcasted_iota(jnp.int32, (1, 128), 1)
        even = lax.rem(lane, 64) < 32
        first = lane < 64
        zero = jnp.zeros((), jnp.bfloat16)
        eye = jnp.where(
            lax.broadcasted_iota(jnp.int32, (seq_loc, 128), 0) == lax.broadcasted_iota(jnp.int32, (seq_loc, 128), 1), 1.0, 0.0
        ).astype(jnp.bfloat16)
        q_copy.wait()

        def attn_body(i, _):
            slot = lax.rem(i, N_KV_SLOTS)
            pltpu.make_async_copy(kv_ring.at[slot], kv_ring.at[slot], kv_sem.at[slot]).wait()

            @pl.when(i + N_KV_SLOTS - 1 < n_b)
            def _():
                start_kv(i + N_KV_SLOTS - 1)

            sl = pl.ds(pl.multiple_of(i * seq_loc, seq_loc), seq_loc)
            for gp in range(4):
                k_t = kv_ring[slot, :, :, gp * 128 : (gp + 1) * 128].reshape(keys, 128)
                v_t = kv_ring[slot, :, :, BLK + gp * 128 : BLK + (gp + 1) * 128].reshape(keys, 128)
                k_ext = jnp.concatenate([k_t, mask_ref[...]], axis=1)
                q_rows = []
                for h in range(4):
                    c0 = gp * BLK + h * 128
                    q_t = q_ref[sl, c0 : c0 + 128]
                    q_rows.append(jnp.concatenate([jnp.where(even, q_t, zero), eye], axis=1))
                    q_rows.append(jnp.concatenate([jnp.where(even, zero, q_t), eye], axis=1))
                s = lax.dot_general(
                    jnp.concatenate(q_rows, axis=0), k_ext, (((1,), (1,)), ((), ())), preferred_element_type=jnp.float32
                )
                m = jnp.max(s, axis=-1, keepdims=True)
                p = jnp.exp(s - m)
                l = jnp.sum(p, axis=-1, keepdims=True)
                o = jnp.dot(p.astype(jnp.bfloat16), v_t, preferred_element_type=jnp.float32)
                o = (o / l).reshape(4, 2, seq_loc, 128)
                for h in range(4):
                    o_ref[gp, sl, h * 128 : (h + 1) * 128] = jnp.where(first, o[h, 0], o[h, 1]).astype(jnp.bfloat16)
            return 0

        lax.fori_loop(0, n_b, attn_body, 0)

        def o_part(j):
            slot = wait_block(j)
            if isinstance(j, int):
                start_block(j + N_ROW_SLOTS - 1)
            else:
                pl.when(j < n_o - 1)(lambda: start_block(j + N_ROW_SLOTS - 1))
            return jnp.dot(o_ref[j], ring[slot], preferred_element_type=jnp.float32)

        acc_ref[...] = o_part(0)

        def o_body(j, _):
            acc_ref[...] += o_part(j)
            return 0

        lax.fori_loop(1, n_o, o_body, 0)
        x_copy.wait()

        def resid_body(i, _):
            sl = pl.ds(pl.multiple_of(i * 64, 64), 64)
            h = (x_ref[sl, :].astype(jnp.float32) + acc_ref[sl, :]).astype(jnp.bfloat16)
            hf = h.astype(jnp.float32)
            ms = jnp.mean(hf * hf, axis=-1, keepdims=True)
            n_ref[sl, :] = (hf * lax.rsqrt(ms + NORM_EPS) * gm_ref[0]).astype(jnp.bfloat16)
            acc_ref[sl, :] = hf
            return 0

        lax.fori_loop(0, rows // 64, resid_body, 0)

        def up_part(slot):
            u_ref[...] = jnp.dot(n_ref[...], up_ring[slot], preferred_element_type=jnp.float32)

        def gelu_part(s):
            a_ref[s] = gelu(u_ref[...]).astype(jnp.bfloat16)

        def down_part(slot, s):
            acc_ref[...] += jnp.dot(a_ref[s], ring[slot], preferred_element_type=jnp.float32)

        def next_down(f):
            slots = [wait_block(f_base + f + s) for s in range(2)]
            for s in range(2):
                start_block(f_base + f + s + N_ROW_SLOTS - 2)
            return slots

        ups = [wait_up(0), wait_up(1)]
        up_part(ups[0])
        gelu_part(0)
        up_part(ups[1])

        def f_body(g, _):
            downs = next_down(2 * g)
            ups = [wait_up(2 * g + 2 + s) for s in range(2)]
            for s in range(2):
                nxt = 2 * g + N_UP_SLOTS + s
                pl.when(nxt < n_f)(functools.partial(start_up, nxt))
            for s in range(2):
                gelu_part(1 - s)
                down_part(downs[s], s)
                up_part(ups[s])
            return 0

        lax.fori_loop(0, n_f // 2 - 1, f_body, 0)
        downs = next_down(n_f - 2)
        gelu_part(1)
        down_part(downs[0], 0)
        down_part(downs[1], 1)
        start_block(q_base + N_ROW_SLOTS - 2)

        def y_body(i, _):
            sl = pl.ds(pl.multiple_of(i * 64, 64), 64)
            y = acc_ref[sl, :].astype(jnp.bfloat16)
            x_ref[sl, :] = y
            if with_qkv:
                yf = y.astype(jnp.float32)
                ms = jnp.mean(yf * yf, axis=-1, keepdims=True)
                n_ref[sl, :] = (yf * lax.rsqrt(ms + NORM_EPS) * ga_ref[0]).astype(jnp.bfloat16)
            return 0

        lax.fori_loop(0, rows // 64, y_body, 0)
        y_copy = pltpu.make_async_copy(x_ref, y_hbm.at[pl.ds(y_row, rows)], out_sem.at[0])
        y_copy.start()
    else:
        x_copy.wait()
        norm_rows(x_ref, ga_ref[0], n_ref, rows)

    if with_qkv:
        reps = rows // seq_loc

        def project(b):
            slot = wait_block(b)
            start_block(b + N_ROW_SLOTS - 1)
            return lax.dot_general(n_ref[...], ring[slot], (((1,), (1,)), ((), ())), preferred_element_type=jnp.float32)

        def rope(t, cos_t, sin_t):
            r3 = t.reshape(reps, seq_loc, 128)
            s3 = pltpu.roll(t, 64, 1).reshape(reps, seq_loc, 128)
            return (r3 * cos_t + s3 * sin_t).reshape(rows, 128).astype(jnp.bfloat16)

        def drain(s, dst):
            pltpu.make_async_copy(st_ref.at[s], dst, out_sem.at[1 + s]).wait()

        def q_body(j, _):
            s = lax.rem(j, 2)

            @pl.when(j >= 2)
            def _():
                drain(s, q_hbm.at[:, pl.ds(0, BLK)])

            res = project(q_base + j)
            for i in range(4):
                st_ref[s, :, i * 128 : (i + 1) * 128] = rope(res[:, i * 128 : (i + 1) * 128], tab_ref[0], tab_ref[1])
            pltpu.make_async_copy(
                st_ref.at[s], q_hbm.at[:, pl.ds(pl.multiple_of(j * BLK, BLK), BLK)], out_sem.at[1 + s]
            ).start()
            return 0

        if with_q:
            lax.fori_loop(0, n_q, q_body, 0)
        if with_kv:
            if with_q:
                drain(0, q_hbm.at[:, pl.ds(0, BLK)])
            kres = project(q_base + n_q)
            for i in range(4):
                st_ref[0, :, i * 128 : (i + 1) * 128] = rope(kres[:, i * 128 : (i + 1) * 128], tab_ref[2], tab_ref[3])
            pltpu.make_async_copy(st_ref.at[0], kv_hbm.at[:, pl.ds(0, BLK)], out_sem.at[1]).start()
            if with_q:
                drain(1, q_hbm.at[:, pl.ds(0, BLK)])
            vres = project(q_base + n_q + 1)
            st_ref[1] = vres.astype(jnp.bfloat16)
            pltpu.make_async_copy(st_ref.at[1], kv_hbm.at[:, pl.ds(BLK, BLK)], out_sem.at[2]).start()
            drain(0, kv_hbm.at[:, pl.ds(0, BLK)])
            drain(1, kv_hbm.at[:, pl.ds(BLK, BLK)])
        else:
            drain(0, q_hbm.at[:, pl.ds(0, BLK)])
            drain(1, q_hbm.at[:, pl.ds(0, BLK)])
    if with_mlp:
        y_copy.wait()


def layer_call(
    layer, x, x_row, rows, attn_in, weights, tables, seq_loc, n_dev, with_q, with_kv, y_rows=None, y_row=0, y_into=None
):
    w_query_t, w_key_t, w_value_t, w_out, w_up, w_down, g_attn, g_mlp = weights
    d_model = x.shape[1]
    ff_dim = w_up.shape[2]
    with_mlp = attn_in is not None
    any_spec = pl.BlockSpec(memory_space=pl.ANY)
    vmem_spec = pl.BlockSpec(memory_space=pltpu.VMEM)
    args, specs = [x], [any_spec]
    outs = []
    flops = 0
    nbytes = 0
    if with_mlp:
        q, kv, mask = attn_in
        args += [q, kv, mask, w_out, w_up, w_down, g_mlp[layer - 1][None]]
        specs += [any_spec] * 2 + [vmem_spec] + [any_spec] * 3 + [vmem_spec]
        outs.append(jax.ShapeDtypeStruct((y_rows or rows, d_model), jnp.bfloat16))
        flops += 2 * rows * d_model * (d_model + 2 * ff_dim) + 16 * rows * d_model * n_dev * seq_loc
        nbytes += 2 * d_model * (d_model + 2 * ff_dim) + 6 * rows * d_model + 2 * kv.size
    if with_q or with_kv:
        args += [w_query_t, w_key_t, w_value_t, g_attn[layer][None], tables]
        specs += [any_spec] * 3 + [vmem_spec] * 2
        n_out = (d_model if with_q else 0) + (2 * BLK if with_kv else 0)
        flops += 2 * rows * d_model * n_out
        nbytes += 2 * d_model * n_out + 2 * rows * n_out
    if with_q:
        outs.append(jax.ShapeDtypeStruct((rows, d_model), jnp.bfloat16))
    if with_kv:
        outs.append(jax.ShapeDtypeStruct((rows, 2 * BLK), jnp.bfloat16))
    aliases = {}
    if y_into is not None:
        aliases = {len(args): 0}
        args.append(y_into)
        specs.append(any_spec)
    scratch = [
        pltpu.VMEM((rows, d_model), jnp.bfloat16),
        pltpu.VMEM((rows, d_model), jnp.bfloat16),
        pltpu.VMEM((N_ROW_SLOTS, BLK, d_model), jnp.bfloat16),
        pltpu.SemaphoreType.DMA((N_ROW_SLOTS,)),
        pltpu.SemaphoreType.DMA,
        pltpu.SemaphoreType.DMA((3,)),
    ]
    if with_mlp:
        scratch += [
            pltpu.VMEM((d_model // BLK, rows, BLK), jnp.bfloat16),
            pltpu.VMEM((rows, d_model), jnp.float32),
            pltpu.VMEM((rows, BLK), jnp.float32),
            pltpu.VMEM((2, rows, BLK), jnp.bfloat16),
            pltpu.VMEM((N_UP_SLOTS, d_model, BLK), jnp.bfloat16),
            pltpu.SemaphoreType.DMA((N_UP_SLOTS,)),
            pltpu.VMEM((rows, d_model), jnp.bfloat16),
            pltpu.SemaphoreType.DMA,
            pltpu.VMEM((N_KV_SLOTS, n_dev, seq_loc, 2 * BLK), jnp.bfloat16),
            pltpu.SemaphoreType.DMA((N_KV_SLOTS,)),
        ]
    if with_q or with_kv:
        scratch.append(pltpu.VMEM((2, rows, BLK), jnp.bfloat16))
    return pl.pallas_call(
        functools.partial(
            layer_kernel, layer, with_mlp, with_q, with_kv, rows, seq_loc, n_dev, d_model, ff_dim, x_row, y_row,
            y_into is not None,
        ),
        out_shape=outs,
        in_specs=specs,
        out_specs=[any_spec] * len(outs),
        scratch_shapes=scratch,
        input_output_aliases=aliases,
        compiler_params=pltpu.CompilerParams(vmem_limit_bytes=60 * 1024 * 1024),
        cost_estimate=pl.CostEstimate(flops=flops, bytes_accessed=nbytes, transcendentals=0),
        name=f"layer_{int(with_mlp)}{int(with_q)}{int(with_kv)}",
    )(*args)


def solution(mesh):
    tok_spec = P(None, ("data", "seq"), None)
    in_specs = (tok_spec, P(("data", "seq"))) + (P(),) * 8

    def device_fn(x_loc, pos_loc, w_query, w_key, w_value, w_out, w_up, w_down, g_attn, g_mlp):
        n_batch, seq_loc, d_model = x_loc.shape
        n_layers = w_query.shape[0]
        n_dev = mesh.shape["seq"]
        scale = w_query.shape[-1] ** -0.5
        cos_t, sin_t = rope_tables(pos_loc, w_query.shape[-1])
        cos4 = jnp.concatenate([cos_t] * 4, axis=-1)
        sin4 = jnp.concatenate([-sin_t, -sin_t, sin_t, sin_t], axis=-1)
        tables = jnp.stack([cos4 * scale, sin4 * scale, cos4, sin4])
        me = lax.axis_index("seq")
        key_pos = jnp.arange(n_dev * seq_loc)
        query_pos = me * seq_loc + jnp.arange(seq_loc)
        mask = jnp.where(key_pos[:, None] <= query_pos[None, :], 0.0, MASK_VALUE)
        mask = jnp.pad(mask, ((0, 0), (0, 128 - seq_loc))).astype(jnp.bfloat16)
        weights = (
            jnp.transpose(w_query, (0, 2, 3, 1)),
            jnp.transpose(w_key, (0, 2, 3, 1)),
            jnp.transpose(w_value, (0, 2, 3, 1)),
            w_out,
            w_up,
            w_down,
            g_attn,
            g_mlp,
        )
        rows = n_batch // N_CHUNKS * seq_loc
        x_all = x_loc.reshape(n_batch * seq_loc, d_model)
        xs = [(x_all, c * rows) for c in range(N_CHUNKS)]
        qs, kvs = [None] * N_CHUNKS, [None] * N_CHUNKS
        call = functools.partial(layer_call, weights=weights, tables=tables, seq_loc=seq_loc, n_dev=n_dev, rows=rows)
        last = None
        for c in range(N_CHUNKS):
            x_c = x_all
            if last is not None:
                x_c, _ = lax.optimization_barrier((x_all, last))
            (kv,) = call(0, x_c, c * rows, attn_in=None, with_q=False, with_kv=True)
            kvs[c] = lax.all_gather(kv, "seq", axis=0, tiled=False)
            last = kv
        for c in range(N_CHUNKS):
            x_c, _ = lax.optimization_barrier((x_all, last))
            (qs[c],) = call(0, x_c, c * rows, attn_in=None, with_q=True, with_kv=False)
            last = qs[c]
        out = None
        for layer in range(1, n_layers + 1):
            for c in range(N_CHUNKS):
                q_c, last = lax.optimization_barrier((qs[c], last))
                attn_in = (q_c, kvs[c], mask)
                if layer < n_layers:
                    y, qs[c], kv = call(layer, *xs[c], attn_in=attn_in, with_q=True, with_kv=True)
                    xs[c] = (y, 0)
                    kvs[c] = lax.all_gather(kv, "seq", axis=0, tiled=False)
                    last = y
                else:
                    (out,) = call(
                        layer, *xs[c], attn_in=attn_in, with_q=False, with_kv=False,
                        y_rows=n_batch * seq_loc, y_row=c * rows, y_into=out,
                    )
                    last = out
        return out.reshape(n_batch, seq_loc, d_model)

    return jax.shard_map(device_fn, mesh=mesh, in_specs=in_specs, out_specs=tok_spec, check_vma=False)
```

time: 579 us -> 554 us (0.957)
  waiting for transfers between devices: 34.7 us -> 15.9 us
    all_gather x6, waiting for transfers between devices: 34.6 us -> 15.8 us  [device_fn(): kvs[c] = lax.all_gather(kv, 'seq', axis=0, tiled=False)]
    pallas_call x14 -> x10, Pallas kernels: 518 us -> 515 us  [layer_call(): pl.pallas_call(functools.partial(layer_kernel, layer, with_mlp, with_q, w...]
  transfers between devices with their start and end apart: 6 -> 6, of which waited for: 1 -> 1; matrix products, arithmetic and copies ran while one was open for 0% -> 0% of each run, Pallas kernels for 75% -> 80%
where the time goes in v2:
time: 554 us; the launch traced here: 550 us
  Pallas kernels  515 us (93%)
  waiting for transfers between devices  15.9 us (3%)
  between operations  13.8 us (2%)
    pallas_call x10, Pallas kernels, layer_call(): pl.pallas_call(functools.partial(layer_kernel, layer, with_mlp, with_q, w...  515 us
    all_gather x6, waiting for transfers between devices, device_fn(): kvs[c] = lax.all_gather(kv, 'seq', axis=0, tiled=False)  15.8 us
  transfers between devices with their start and end apart: 6, of which 1 were waited for; matrix products, arithmetic and copies ran while one was open for 0% of the time, Pallas kernels for 80%

profile of v2, /device:TPU:0, one launch (start us, length us, event | category | flops | bytes accessed | tf_op | source)
XLA Modules:
  0.0 549.9 jit_solution(2575368674924793245)
XLA Ops:
  6.5 0.7 convert_element_type.6
  7.2 1.5 fusion.5
  8.7 0.2 fusion.3
  8.9 0.1 maximum_multiply_fusion
  9.0 0.1 maximum_bitcast_fusion
  9.1 0.7 pad_maximum_fusion.refs_5_.refs_12_
  9.8 8.8 %layer_001.2 = bf16[512,1024]{1,0:T(8,128)(2,1)} custom-call(bf16[1024,2048]{1,0:T(8,128)(2,1)} %bitcast.45, bf16[3,32,64,2048]{3,2,1,0:T(8,128)(2,1)} %bitcast.21, bf16[3,8,64,2048]{3,2,1,0:T(8,128)(2,1)} %bitcast.29, bf16[3,8,64,2048]{3,2,1,0:T(8,128)(2,1)} %bitcast.37, f32[1,2048]{1,0:T(1,128)} %get-tuple-element.51.refs_4_, ...), custom_call_target="tpu_custom_call" | custom-call | flops 2147483648 | bytes 5242880 | tf_op jit(solution)/shard_map/layer_001/pallas_call | solution.py:417
  18.6 0.0 all-gather.15.cloned.1.call-start
  18.7 8.8 %layer_001.3 = bf16[512,1024]{1,0:T(8,128)(2,1)} custom-call(bf16[1024,2048]{1,0:T(8,128)(2,1)} %bitcast.46, bf16[3,32,64,2048]{3,2,1,0:T(8,128)(2,1)} %bitcast.22, bf16[3,8,64,2048]{3,2,1,0:T(8,128)(2,1)} %bitcast.30, bf16[3,8,64,2048]{3,2,1,0:T(8,128)(2,1)} %bitcast.38, f32[1,2048]{1,0:T(1,128)} %get-tuple-element.51.refs_4_, ...), custom_call_target="tpu_custom_call" | custom-call | flops 2147483648 | bytes 5242880 | tf_op jit(solution)/shard_map/layer_001/pallas_call | solution.py:417
  27.5 0.4 all-gather.17.cloned.1.call-start
  27.9 13.4 %layer_010.2.refs_1_ = bf16[512,2048]{1,0:T(8,128)(2,1)} custom-call(bf16[1024,2048]{1,0:T(8,128)(2,1)} %bitcast.47, bf16[3,32,64,2048]{3,2,1,0:T(8,128)(2,1)} %bitcast.23, bf16[3,8,64,2048]{3,2,1,0:T(8,128)(2,1)} %bitcast.31, bf16[3,8,64,2048]{3,2,1,0:T(8,128)(2,1)} %bitcast.39, f32[1,2048]{1,0:T(1,128)} %get-tuple-element.51.refs_4_, ...), custom_call_target="tpu_custom_call" | custom-call | flops 4294967296 | bytes 10485760 | tf_op jit(solution)/shard_map/layer_010/pallas_call | solution.py:417
  41.3 13.4 %layer_010.3.refs_1_ = bf16[512,2048]{1,0:T(8,128)(2,1)} custom-call(bf16[1024,2048]{1,0:T(8,128)(2,1)} %bitcast.48, bf16[3,32,64,2048]{3,2,1,0:T(8,128)(2,1)} %bitcast.24, bf16[3,8,64,2048]{3,2,1,0:T(8,128)(2,1)} %bitcast.32, bf16[3,8,64,2048]{3,2,1,0:T(8,128)(2,1)} %bitcast.40, f32[1,2048]{1,0:T(1,128)} %get-tuple-element.51.refs_4_, ...), custom_call_target="tpu_custom_call" | custom-call | flops 4294967296 | bytes 10485760 | tf_op jit(solution)/shard_map/layer_010/pallas_call | solution.py:417
  54.8 0.7 pad.5.refs_3_
  55.4 0.6 fusion.4
  56.1 15.7 %all-gather.13.cloned.1.call-done = bf16[4096,1024]{1,0:T(8,128)(2,1)} async-done(((bf16[512,1024]{1,0:T(8,128)(2,1)}), bf16[4096,1024]{1,0:T(8,128)(2,1)}) %all-gather.13.cloned.1.call-update) | async-done | bytes 8388624 | tf_op jit(solution)/shard_map/all_gather | solution.py:472
  71.7 93.0 %layer_111.4 = (bf16[512,2048]{1,0:T(8,128)(2,1)}, bf16[512,2048]{1,0:T(8,128)(2,1)}, bf16[512,1024]{1,0:T(8,128)(2,1)}) custom-call(bf16[1024,2048]{1,0:T(8,128)(2,1)} %bitcast.49, bf16[512,2048]{1,0:T(8,128)(2,1)} %layer_010.2.refs_1_, bf16[8,512,1024]{2,1,0:T(8,128)(2,1)} %bitcast.52, bf16[512,128]{1,0:T(8,128)(2,1)} %pad.5.refs_3_, ...), custom_call_target="tpu_custom_call" | custom-call | flops 53687091200 | bytes 105906176 | tf_op jit(solution)/shard_map/layer_111/pallas_call | solution.py:417
  164.7 0.0 all-gather.19.cloned.1.call-start
  164.8 79.6 %layer_111.5 = (bf16[512,2048]{1,0:T(8,128)(2,1)}, bf16[512,2048]{1,0:T(8,128)(2,1)}, bf16[512,1024]{1,0:T(8,128)(2,1)}) custom-call(bf16[1024,2048]{1,0:T(8,128)(2,1)} %bitcast.50, bf16[512,2048]{1,0:T(8,128)(2,1)} %layer_010.3.refs_1_, bf16[8,512,1024]{2,1,0:T(8,128)(2,1)} %bitcast.51, bf16[512,128]{1,0:T(8,128)(2,1)} %pad.5.refs_3_, ...), custom_call_target="tpu_custom_call" | custom-call | flops 53687091200 | bytes 105906176 | tf_op jit(solution)/shard_map/layer_111/pallas_call | solution.py:417
  244.4 0.0 all-gather.21.cloned.1.call-start
  244.5 80.1 %layer_111.6 = (bf16[512,2048]{1,0:T(8,128)(2,1)}, bf16[512,2048]{1,0:T(8,128)(2,1)}, bf16[512,1024]{1,0:T(8,128)(2,1)}) custom-call(bf16[512,2048]{1,0:T(8,128)(2,1)} %get-tuple-element.30.refs_0_, bf16[512,2048]{1,0:T(8,128)(2,1)} %get-tuple-element.35.refs_1_, bf16[8,512,1024]{2,1,0:T(8,128)(2,1)} %bitcast.54, bf16[512,128]{1,0:T(8,128)(2,1)} %pad.5.refs_3_, ...), custom_call_target="tpu_custom_call" | custom-call | flops 53687091200 | bytes 105906176 | tf_op jit(solution)/shard_map/layer_111/pallas_call | solution.py:417
  324.7 0.0 all-gather.23.cloned.1.call-start
  324.7 80.0 %layer_111.7 = (bf16[512,2048]{1,0:T(8,128)(2,1)}, bf16[512,2048]{1,0:T(8,128)(2,1)}, bf16[512,1024]{1,0:T(8,128)(2,1)}) custom-call(bf16[512,2048]{1,0:T(8,128)(2,1)} %get-tuple-element.32.refs_0_, bf16[512,2048]{1,0:T(8,128)(2,1)} %get-tuple-element.38.refs_1_, bf16[8,512,1024]{2,1,0:T(8,128)(2,1)} %bitcast.53, bf16[512,128]{1,0:T(8,128)(2,1)} %pad.5.refs_3_, ...), custom_call_target="tpu_custom_call" | custom-call | flops 53687091200 | bytes 105906176 | tf_op jit(solution)/shard_map/layer_111/pallas_call | solution.py:417
  404.8 69.1 %layer_100.2.refs_8_ = bf16[1024,2048]{1,0:T(8,128)(2,1)} custom-call(bf16[512,2048]{1,0:T(8,128)(2,1)} %get-tuple-element.37.refs_0_, bf16[512,2048]{1,0:T(8,128)(2,1)} %get-tuple-element.43.refs_1_, bf16[8,512,1024]{2,1,0:T(8,128)(2,1)} %bitcast.55, bf16[512,128]{1,0:T(8,128)(2,1)} %pad.5.refs_3_, bf16[3,32,64,2048]{3,2,1,0:T(8,128)(2,1)} %refs_4_.11, ...), custom_call_target="tpu_custom_call" | custom-call | flops 47244640256 | bytes 90177536 | tf_op jit(solution)/shard_map/layer_100/pallas_call | solution.py:417
  473.9 68.9 %layer_100.3 = bf16[1024,2048]{1,0:T(8,128)(2,1)} custom-call(bf16[512,2048]{1,0:T(8,128)(2,1)} %get-tuple-element.40.refs_0_, bf16[512,2048]{1,0:T(8,128)(2,1)} %get-tuple-element.45.refs_1_, bf16[8,512,1024]{2,1,0:T(8,128)(2,1)} %bitcast.56, bf16[512,128]{1,0:T(8,128)(2,1)} %pad.5.refs_3_, ...), custom_call_target="tpu_custom_call", output_to_operand_aliasing={{}: (8, {})} | custom-call | flops 47244640256 | bytes 90177536 | tf_op jit(solution)/shard_map/layer_100/pallas_call | solution.py:417
  (17 shorter events, 0.3 us)
Async XLA Ops:
  6.5 65.2 %all-gather.13.cloned.1.call-start = ((), (), s32[]{:S(2)}) async-start(), calls=%async_computation | async-start | bytes 9437184 | tf_op jit(solution)/shard_map/all_gather | solution.py:472
  18.6 146.2 %all-gather.15.cloned.1.call-start = ((), (), s32[]{:S(2)}) async-start(), calls=%async_computation.1 | async-start | bytes 9437184 | tf_op jit(solution)/shard_map/all_gather | solution.py:472
  27.5 217.0 %all-gather.17.cloned.1.call-start = ((), (), s32[]{:S(2)}) async-start(), calls=%async_computation.2 | async-start | bytes 9437184 | tf_op jit(solution)/shard_map/all_gather | solution.py:486
  41.3 14.1 %copy-start = (f32[3,2048]{1,0:T(4,128)S(1)}, f32[3,2048]{1,0:T(4,128)}, u32[]{:S(2)}) copy-start(f32[3,2048]{1,0:T(4,128)} %param.19) | copy-start | bytes 73732
  164.7 160.0 %all-gather.19.cloned.1.call-start = ((), (), s32[]{:S(2)}) async-start(), calls=%async_computation.3 | async-start | bytes 9437184 | tf_op jit(solution)/shard_map/all_gather | solution.py:486
  244.4 160.4 %all-gather.21.cloned.1.call-start = ((), (), s32[]{:S(2)}) async-start(), calls=%async_computation.4 | async-start | bytes 9437184 | tf_op jit(solution)/shard_map/all_gather | solution.py:486
  324.7 149.2 %all-gather.23.cloned.1.call-start = ((), (), s32[]{:S(2)}) async-start(), calls=%async_computation.5 | async-start | bytes 9437184 | tf_op jit(solution)/shard_map/all_gather | solution.py:486
Sparse Core Ops, SparseCore 0:
  18.7 52.9 all-gather.12
  73.6 50.1 all-gather.14
  164.8 50.1 all-gather.16
  244.5 50.1 all-gather.18
  324.8 50.1 all-gather.20
  404.9 50.1 all-gather.22

commit v3 on v2

--- a/solution.py
+++ b/solution.py
@@ -167,12 +167,10 @@
         q_copy.start()
         for i in range(N_KV_SLOTS - 1):
             start_kv(i)
-    x_copy.start()
-    for b in range(min(N_ROW_SLOTS - 1, n_blocks)):
-        start_block(b)
-    if with_mlp:
-        for f in range(N_UP_SLOTS):
-            start_up(f)
+    if not with_mlp:
+        x_copy.start()
+        for b in range(min(N_ROW_SLOTS - 1, n_blocks)):
+            start_block(b)
 
     if with_mlp:
         keys = n_dev * seq_loc
@@ -192,6 +190,10 @@
             @pl.when(i + N_KV_SLOTS - 1 < n_b)
             def _():
                 start_kv(i + N_KV_SLOTS - 1)
+
+            pl.when(i == 0)(x_copy.start)
+            pl.when(jnp.logical_and(i >= 1, i < N_ROW_SLOTS))(lambda: start_block(i - 1))
+            pl.when(i >= n_b - N_UP_SLOTS)(lambda: start_up(i - (n_b - N_UP_SLOTS)))
 
             sl = pl.ds(pl.multiple_of(i * seq_loc, seq_loc), seq_loc)
             for gp in range(4):
@@ -229,7 +231,8 @@
         acc_ref[...] = o_part(0)
 
         def o_body(j, _):
-            acc_ref[...] += o_part(j)
+            part = o_part(j)
+            acc_ref[...] += part
             return 0
 
         lax.fori_loop(1, n_o, o_body, 0)
@@ -240,7 +243,7 @@
             h = (x_ref[sl, :].astype(jnp.float32) + acc_ref[sl, :]).astype(jnp.bfloat16)
             hf = h.astype(jnp.float32)
             ms = jnp.mean(hf * hf, axis=-1, keepdims=True)
-            n_ref[sl, :] = (hf * lax.rsqrt(ms + NORM_EPS) * gm_ref[0]).astype(jnp.bfloat16)
+            n_ref[sl, :] = (hf * lax.rsqrt(ms + NORM_EPS) * gm_ref[mlp_layer]).astype(jnp.bfloat16)
             acc_ref[sl, :] = hf
             return 0
 
@@ -292,7 +295,7 @@
             if with_qkv:
                 yf = y.astype(jnp.float32)
                 ms = jnp.mean(yf * yf, axis=-1, keepdims=True)
-                n_ref[sl, :] = (yf * lax.rsqrt(ms + NORM_EPS) * ga_ref[0]).astype(jnp.bfloat16)
+                n_ref[sl, :] = (yf * lax.rsqrt(ms + NORM_EPS) * ga_ref[layer]).astype(jnp.bfloat16)
             return 0
 
         lax.fori_loop(0, rows // 64, y_body, 0)
@@ -300,7 +303,7 @@
         y_copy.start()
     else:
         x_copy.wait()
-        norm_rows(x_ref, ga_ref[0], n_ref, rows)
+        norm_rows(x_ref, ga_ref[layer], n_ref, rows)
 
     if with_qkv:
         reps = rows // seq_loc
@@ -371,13 +374,13 @@
     nbytes = 0
     if with_mlp:
         q, kv, mask = attn_in
-        args += [q, kv, mask, w_out, w_up, w_down, g_mlp[layer - 1][None]]
+        args += [q, kv, mask, w_out, w_up, w_down, g_mlp]
         specs += [any_spec] * 2 + [vmem_spec] + [any_spec] * 3 + [vmem_spec]
         outs.append(jax.ShapeDtypeStruct((y_rows or rows, d_model), jnp.bfloat16))
         flops += 2 * rows * d_model * (d_model + 2 * ff_dim) + 16 * rows * d_model * n_dev * seq_loc
         nbytes += 2 * d_model * (d_model + 2 * ff_dim) + 6 * rows * d_model + 2 * kv.size
     if with_q or with_kv:
-        args += [w_query_t, w_key_t, w_value_t, g_attn[layer][None], tables]
+        args += [w_query_t, w_key_t, w_value_t, g_attn, tables]
         specs += [any_spec] * 3 + [vmem_spec] * 2
         n_out = (d_model if with_q else 0) + (2 * BLK if with_kv else 0)
         flops += 2 * rows * d_model * n_out

time: 554 us -> 505 us (0.912)
  Pallas kernels: 515 us -> 467 us
    pallas_call x10, Pallas kernels: 515 us -> 467 us  [layer_call(): pl.pallas_call(functools.partial(layer_kernel, layer, with_mlp, with_q, w...]
  transfers between devices with their start and end apart: 6 -> 6, of which waited for: 1 -> 1; matrix products, arithmetic and copies ran while one was open for 0% -> 0% of each run, Pallas kernels for 80% -> 79%
where the time goes in v3:
time: 505 us; the launch traced here: 501 us
  Pallas kernels  467 us (92%)
  waiting for transfers between devices  16.7 us (3%)
  between operations  13.9 us (3%)
    pallas_call x10, Pallas kernels, layer_call(): pl.pallas_call(functools.partial(layer_kernel, layer, with_mlp, with_q, w...  467 us
    all_gather x6, waiting for transfers between devices, device_fn(): kvs[c] = lax.all_gather(kv, 'seq', axis=0, tiled=False)  16.6 us
  transfers between devices with their start and end apart: 6, of which 1 were waited for; matrix products, arithmetic and copies ran while one was open for 0% of the time, Pallas kernels for 79%

profile of v3, /device:TPU:0, one launch (start us, length us, event | category | flops | bytes accessed | tf_op | source)
XLA Modules:
  0.0 500.8 jit_solution(14302976708509448618)
XLA Ops:
  6.5 0.7 convert_element_type.6
  7.2 0.2 fusion.3
  7.4 0.1 maximum_multiply_fusion
  7.5 0.1 maximum_bitcast_fusion
  7.7 0.7 pad_maximum_fusion.refs_5_.refs_12_
  8.3 8.8 %layer_001.2 = bf16[512,1024]{1,0:T(8,128)(2,1)} custom-call(bf16[1024,2048]{1,0:T(8,128)(2,1)} %bitcast.45, bf16[3,32,64,2048]{3,2,1,0:T(8,128)(2,1)} %bitcast.21, bf16[3,8,64,2048]{3,2,1,0:T(8,128)(2,1)} %bitcast.29, bf16[3,8,64,2048]{3,2,1,0:T(8,128)(2,1)} %bitcast.37, f32[3,2048]{1,0:T(4,128)} %refs_11_.7, f32[4,64,128]{2,1,0:T(8,128)} %pad_maximum_fusion.refs_5_.refs_12_), custom_call_target="tpu_custom_call" | custom-call | flops 2147483648 | bytes 5242880 | tf_op jit(solution)/shard_map/layer_001/pallas_call | solution.py:420
  17.2 0.0 all-gather.15.cloned.1.call-start
  17.2 8.8 %layer_001.3 = bf16[512,1024]{1,0:T(8,128)(2,1)} custom-call(bf16[1024,2048]{1,0:T(8,128)(2,1)} %bitcast.46, bf16[3,32,64,2048]{3,2,1,0:T(8,128)(2,1)} %bitcast.22, bf16[3,8,64,2048]{3,2,1,0:T(8,128)(2,1)} %bitcast.30, bf16[3,8,64,2048]{3,2,1,0:T(8,128)(2,1)} %bitcast.38, f32[3,2048]{1,0:T(4,128)} %refs_11_.7, f32[4,64,128]{2,1,0:T(8,128)} %pad_maximum_fusion.refs_5_.refs_12_), custom_call_target="tpu_custom_call" | custom-call | flops 2147483648 | bytes 5242880 | tf_op jit(solution)/shard_map/layer_001/pallas_call | solution.py:420
  26.0 0.2 all-gather.17.cloned.1.call-start
  26.3 13.4 %layer_010.2.refs_1_ = bf16[512,2048]{1,0:T(8,128)(2,1)} custom-call(bf16[1024,2048]{1,0:T(8,128)(2,1)} %bitcast.47, bf16[3,32,64,2048]{3,2,1,0:T(8,128)(2,1)} %bitcast.23, bf16[3,8,64,2048]{3,2,1,0:T(8,128)(2,1)} %bitcast.31, bf16[3,8,64,2048]{3,2,1,0:T(8,128)(2,1)} %bitcast.39, f32[3,2048]{1,0:T(4,128)} %refs_11_.7, ...), custom_call_target="tpu_custom_call" | custom-call | flops 4294967296 | bytes 10485760 | tf_op jit(solution)/shard_map/layer_010/pallas_call | solution.py:420
  39.7 13.4 %layer_010.3.refs_1_ = bf16[512,2048]{1,0:T(8,128)(2,1)} custom-call(bf16[1024,2048]{1,0:T(8,128)(2,1)} %bitcast.48, bf16[3,32,64,2048]{3,2,1,0:T(8,128)(2,1)} %bitcast.24, bf16[3,8,64,2048]{3,2,1,0:T(8,128)(2,1)} %bitcast.32, bf16[3,8,64,2048]{3,2,1,0:T(8,128)(2,1)} %bitcast.40, f32[3,2048]{1,0:T(4,128)} %refs_11_.7, ...), custom_call_target="tpu_custom_call" | custom-call | flops 4294967296 | bytes 10485760 | tf_op jit(solution)/shard_map/layer_010/pallas_call | solution.py:420
  53.1 0.7 pad.5.refs_3_
  53.8 16.5 %all-gather.13.cloned.1.call-done = bf16[4096,1024]{1,0:T(8,128)(2,1)} async-done(((bf16[512,1024]{1,0:T(8,128)(2,1)}), bf16[4096,1024]{1,0:T(8,128)(2,1)}) %all-gather.13.cloned.1.call-update) | async-done | bytes 8388624 | tf_op jit(solution)/shard_map/all_gather | solution.py:475
  70.3 74.3 %layer_111.4 = (bf16[512,2048]{1,0:T(8,128)(2,1)}, bf16[512,2048]{1,0:T(8,128)(2,1)}, bf16[512,1024]{1,0:T(8,128)(2,1)}) custom-call(bf16[1024,2048]{1,0:T(8,128)(2,1)} %bitcast.49, bf16[512,2048]{1,0:T(8,128)(2,1)} %layer_010.2.refs_1_, bf16[8,512,1024]{2,1,0:T(8,128)(2,1)} %bitcast.52, bf16[512,128]{1,0:T(8,128)(2,1)} %pad.5.refs_3_, ...), custom_call_target="tpu_custom_call" | custom-call | flops 53687091200 | bytes 105906176 | tf_op jit(solution)/shard_map/layer_111/pallas_call | solution.py:420
  144.6 0.0 all-gather.19.cloned.1.call-start
  144.7 73.9 %layer_111.5 = (bf16[512,2048]{1,0:T(8,128)(2,1)}, bf16[512,2048]{1,0:T(8,128)(2,1)}, bf16[512,1024]{1,0:T(8,128)(2,1)}) custom-call(bf16[1024,2048]{1,0:T(8,128)(2,1)} %bitcast.50, bf16[512,2048]{1,0:T(8,128)(2,1)} %layer_010.3.refs_1_, bf16[8,512,1024]{2,1,0:T(8,128)(2,1)} %bitcast.51, bf16[512,128]{1,0:T(8,128)(2,1)} %pad.5.refs_3_, ...), custom_call_target="tpu_custom_call" | custom-call | flops 53687091200 | bytes 105906176 | tf_op jit(solution)/shard_map/layer_111/pallas_call | solution.py:420
  218.7 0.0 all-gather.21.cloned.1.call-start
  218.8 74.5 %layer_111.6 = (bf16[512,2048]{1,0:T(8,128)(2,1)}, bf16[512,2048]{1,0:T(8,128)(2,1)}, bf16[512,1024]{1,0:T(8,128)(2,1)}) custom-call(bf16[512,2048]{1,0:T(8,128)(2,1)} %get-tuple-element.30.refs_0_, bf16[512,2048]{1,0:T(8,128)(2,1)} %get-tuple-element.35.refs_1_, bf16[8,512,1024]{2,1,0:T(8,128)(2,1)} %bitcast.54, bf16[512,128]{1,0:T(8,128)(2,1)} %pad.5.refs_3_, ...), custom_call_target="tpu_custom_call" | custom-call | flops 53687091200 | bytes 105906176 | tf_op jit(solution)/shard_map/layer_111/pallas_call | solution.py:420
  293.3 0.0 all-gather.23.cloned.1.call-start
  293.4 74.2 %layer_111.7 = (bf16[512,2048]{1,0:T(8,128)(2,1)}, bf16[512,2048]{1,0:T(8,128)(2,1)}, bf16[512,1024]{1,0:T(8,128)(2,1)}) custom-call(bf16[512,2048]{1,0:T(8,128)(2,1)} %get-tuple-element.32.refs_0_, bf16[512,2048]{1,0:T(8,128)(2,1)} %get-tuple-element.38.refs_1_, bf16[8,512,1024]{2,1,0:T(8,128)(2,1)} %bitcast.53, bf16[512,128]{1,0:T(8,128)(2,1)} %pad.5.refs_3_, ...), custom_call_target="tpu_custom_call" | custom-call | flops 53687091200 | bytes 105906176 | tf_op jit(solution)/shard_map/layer_111/pallas_call | solution.py:420
  367.6 0.0 all-gather.21.cloned.1.call-done
  367.6 63.1 %layer_100.2.refs_8_ = bf16[1024,2048]{1,0:T(8,128)(2,1)} custom-call(bf16[512,2048]{1,0:T(8,128)(2,1)} %get-tuple-element.37.refs_0_, bf16[512,2048]{1,0:T(8,128)(2,1)} %get-tuple-element.43.refs_1_, bf16[8,512,1024]{2,1,0:T(8,128)(2,1)} %bitcast.55, bf16[512,128]{1,0:T(8,128)(2,1)} %pad.5.refs_3_, bf16[3,32,64,2048]{3,2,1,0:T(8,128)(2,1)} %refs_4_.19, ...), custom_call_target="tpu_custom_call" | custom-call | flops 47244640256 | bytes 90177536 | tf_op jit(solution)/shard_map/layer_100/pallas_call | solution.py:420
  430.7 0.0 all-gather.23.cloned.1.call-done
  430.8 62.9 %layer_100.3 = bf16[1024,2048]{1,0:T(8,128)(2,1)} custom-call(bf16[512,2048]{1,0:T(8,128)(2,1)} %get-tuple-element.40.refs_0_, bf16[512,2048]{1,0:T(8,128)(2,1)} %get-tuple-element.45.refs_1_, bf16[8,512,1024]{2,1,0:T(8,128)(2,1)} %bitcast.56, bf16[512,128]{1,0:T(8,128)(2,1)} %pad.5.refs_3_, ...), custom_call_target="tpu_custom_call", output_to_operand_aliasing={{}: (8, {})} | custom-call | flops 47244640256 | bytes 90177536 | tf_op jit(solution)/shard_map/layer_100/pallas_call | solution.py:420
  (13 shorter events, 0.2 us)
Async XLA Ops:
  6.5 63.7 %all-gather.13.cloned.1.call-start = ((), (), s32[]{:S(2)}) async-start(), calls=%async_computation | async-start | bytes 9437184 | tf_op jit(solution)/shard_map/all_gather | solution.py:475
  17.2 127.5 %all-gather.15.cloned.1.call-start = ((), (), s32[]{:S(2)}) async-start(), calls=%async_computation.1 | async-start | bytes 9437184 | tf_op jit(solution)/shard_map/all_gather | solution.py:475
  26.0 192.7 %all-gather.17.cloned.1.call-start = ((), (), s32[]{:S(2)}) async-start(), calls=%async_computation.2 | async-start | bytes 9437184 | tf_op jit(solution)/shard_map/all_gather | solution.py:489
  144.6 148.7 %all-gather.19.cloned.1.call-start = ((), (), s32[]{:S(2)}) async-start(), calls=%async_computation.3 | async-start | bytes 9437184 | tf_op jit(solution)/shard_map/all_gather | solution.py:489
  218.7 148.9 %all-gather.21.cloned.1.call-start = ((), (), s32[]{:S(2)}) async-start(), calls=%async_computation.4 | async-start | bytes 9437184 | tf_op jit(solution)/shard_map/all_gather | solution.py:489
  293.3 137.5 %all-gather.23.cloned.1.call-start = ((), (), s32[]{:S(2)}) async-start(), calls=%async_computation.5 | async-start | bytes 9437184 | tf_op jit(solution)/shard_map/all_gather | solution.py:489
Sparse Core Ops, SparseCore 0:
  17.3 52.9 all-gather.12
  72.1 50.1 all-gather.14
  144.8 50.1 all-gather.16
  218.8 50.1 all-gather.18
  293.4 50.2 all-gather.20
  367.7 50.1 all-gather.22
